TPU v7x, 512 devices: a whole 4x8x8 slice. The times are simulated.
512 devices in a mesh: dp: 32 (over z, x), mp: 16 (over y, core).
Axes of the slice: x: 4, y: 8, z: 8, core: 2. Of those that a mesh axis runs over, the one named last changes fastest.
Arguments:
- activations: bfloat16 [4096, 4096], P('dp'), may hold values from -6 to 6
- cotangents: bfloat16 [4096, 16384], P('dp', 'mp'), may hold values from -1200 to 1200
- owners: int32 [16], replicated, may hold values from 0 to 31, as said below
Outputs:
- update: bfloat16 [4096, 16384], P('dp', 'mp')
- roots: float32 [16384, 8192], P('dp', 'mp')
- graft: float32 [], replicated
Inputs may be any that keep to these rules, and one draw needn't show every extreme that they name: The left root of block b is computed at dp index owners[b] and its right root at owners[b] with its lowest bit flipped; every dp index computes exactly one root.
All inputs are finite; a program needn't handle non-finite values.
Results may differ from a plain program's by a relative error of at most 0.00045.
Values may be sent and summed in bfloat16 or wider, within the bound.
A program may use at most 64 MiB of HBM per device.

v0:
```python
import math

import jax
import jax.numpy as jnp
from jax import lax
from jax.sharding import Mesh
from jax.sharding import PartitionSpec as P

B = 512
CB = 2
ITERS = 3
DP = ("dp_0", "dp_1")
DP_MP = ("dp_0", "dp_1", "mp_0", "mp_1")
MP = ("mp_0", "mp_1")


def partner_2(value, axis, bit):
    return lax.ppermute(value, axis, [(i, i ^ 1 << bit) for i in range(lax.axis_size(axis))])


def one_axis_at_a_time(value, axes):
    for axis in axes:
        value = lax.psum(value, axis)
    return value


def product(left, right):
    return jnp.dot(left, right, precision=lax.Precision.HIGHEST, preferred_element_type=jnp.float32)


def statistic_of(operand):
    gram = product(operand, operand.T)
    ridge = 0.1 * (jnp.sum(operand * operand) / operand.shape[0] + 1.0)
    return gram + ridge * jnp.eye(operand.shape[0], dtype=jnp.float32)


def inverse_root(statistic):
    eye_matrix = jnp.eye(statistic.shape[0], dtype=jnp.float32)
    magnitude = jnp.sqrt(jnp.sum(statistic * statistic))
    current = statistic / magnitude
    result = eye_matrix
    for step in range(ITERS):
        factor = (5.0 * eye_matrix - current) * 0.25
        if step == 0:
            result = factor * magnitude ** (-0.25)
        else:
            result = product(result, factor)
        if step + 1 < ITERS:
            square = product(factor, factor)
            current = product(product(square, square), current)
    return result


def half_squares(matrix, upper_half):
    row_ids = jnp.arange(matrix.shape[0], dtype=jnp.int32)
    in_half = (row_ids < matrix.shape[0] // 2) == upper_half
    return jnp.sum(jnp.where(in_half[:, None], matrix * matrix, 0.0), axis=0)


def on_device(activations, cotangents, owners):
    my_index = lax.axis_index(DP)
    dp_count = lax.axis_size(DP)
    local_tokens = activations.shape[0]
    row_blocks = activations.shape[1] // B
    block_count = owners.shape[0]
    dest_index = jnp.arange(dp_count, dtype=jnp.int32)
    partner = owners + 1 - 2 * (owners % 2)
    left_match = owners[None, :] == dest_index[:, None]
    right_match = partner[None, :] == dest_index[:, None]
    block_ids = jnp.arange(block_count, dtype=jnp.int32)
    owned = jnp.sum(jnp.where(left_match | right_match, block_ids[None, :], 0), axis=1)
    left_dest = jnp.any(left_match, axis=1)
    row_dest = owned // CB
    col_dest = owned % CB
    my_block = owned[my_index]
    my_left = left_dest[my_index]
    token_rows = jnp.take(activations.reshape(local_tokens, row_blocks, B), row_dest, axis=1)
    cotangent_rows = jnp.take(cotangents.reshape(local_tokens, CB, B), col_dest, axis=1)
    mixed = jnp.where(left_dest[None, :, None], token_rows, cotangent_rows)
    received = lax.all_to_all(mixed, DP, split_axis=1, concat_axis=0, tiled=True)[:, 0, :]
    partner_part = partner_2(received, DP, 0)
    inputs_block = jnp.where(my_left, received, partner_part)
    outputs_block = jnp.where(my_left, partner_part, received)
    all_tokens = inputs_block.shape[0]
    gradient = lax.dot_general(
        inputs_block, outputs_block, (((0,), (0,)), ((), ())), preferred_element_type=jnp.float32
    ) / math.sqrt(all_tokens)
    grad_share = half_squares(gradient, my_left)
    grad_total = jnp.sum(one_axis_at_a_time(grad_share, DP_MP))
    oriented = jnp.where(my_left, gradient, gradient.T)
    root = inverse_root(statistic_of(oriented))
    other_root = partner_2(root, DP, 0)
    left_root = jnp.where(my_left, root, other_root)
    right_root = jnp.where(my_left, other_root, root)
    preconditioned = product(left_root, product(gradient, right_root))
    precond_share = half_squares(preconditioned, my_left)
    precond_total = jnp.sum(one_axis_at_a_time(precond_share, DP_MP))
    graft = jnp.sqrt(grad_total / jnp.maximum(precond_total, 1.0))
    scaled = jnp.where(my_left, graft * preconditioned, 0.0).astype(jnp.bfloat16)
    dest_rows = activations.shape[1] // dp_count
    pieces = scaled.reshape(B // dest_rows, dest_rows, B)
    outgoing = jnp.zeros((dp_count, dest_rows, B), jnp.bfloat16)
    first_dest = my_block // CB * (B // dest_rows)
    outgoing = lax.dynamic_update_slice(outgoing, pieces, (first_dest, jnp.int32(0), jnp.int32(0)))
    incoming = lax.all_to_all(outgoing, DP, split_axis=0, concat_axis=0, tiled=True)
    selector = (
        (col_dest[:, None] == jnp.arange(CB, dtype=jnp.int32)[None, :]) & left_dest[:, None]
    ).astype(jnp.bfloat16)
    update = jnp.einsum("srb,sc->rcb", incoming, selector, preferred_element_type=jnp.float32)
    update = update.reshape(dest_rows, CB * B).astype(jnp.bfloat16)
    return (update, root, graft)


def solution(mesh):
    finer = Mesh(mesh.devices.reshape(8, 4, 8, 2), ("dp_0", "dp_1", "mp_0", "mp_1"))
    return jax.shard_map(
        on_device,
        mesh=finer,
        in_specs=(P(DP, None), P(DP, MP), P()),
        out_specs=(P(DP, MP), P(DP, MP), P()),
        check_vma=False,
    )
```

profile of v0, /device:TPU:1, one launch (start us, length us, event | category | flops | bytes accessed | tf_op | source)
XLA Modules:
  0.0 430.1 jit_solution(10846296032719077364)
XLA Ops:
  5.4 2.8 gather_fusion
  8.2 2.7 gather_fusion.1
  10.9 3.9 select_bitcast_fusion
  14.8 107.2 %all_to_all.20 = bf16[128,32,512]{2,0,1:T(8,128)(2,1)} all-to-all(bf16[128,32,512]{2,0,1:T(8,128)(2,1)S(1)} %select_bitcast_fusion), channel_id=1, replica_groups=mesh['dp_0'=8,'dp_1'=4,'mp_0'=8,'mp_1'=2] {'dp_0','dp_1'}, dimensions={1} | all-to-all | bytes 8388608 | tf_op jit(solution)/shard_map/all_to_all | solution.py:80
  122.0 3.9 collective-permute-start
  127.2 87.1 %collective-permute-done = bf16[4096,512]{1,0:T(8,128)(2,1)} collective-permute-done((bf16[4096,512]{1,0:T(8,128)(2,1)}, bf16[4096,512]{1,0:T(8,128)(2,1)}, u32[]{:S(2)}, u32[]{:S(2)}) %collective-permute-start) | collective-permute-done | bytes 4194336 | tf_op jit(solution)/shard_map/ppermute | solution.py:18
  214.2 6.5 %fusion.7 = f32[512,512]{1,0:T(8,128)S(1)} fusion(bf16[4096,512]{1,0:T(8,128)(2,1)} %collective-permute-done, bf16[4096,512]{1,0:T(8,128)(2,1)} %bitcast.10, pred[]{:T(512)} %bitcast.1), kind=kOutput, calls=%fused_computation.14 | convolution fusion | flops 2151940096 | bytes 9437185 | tf_op jit(solution)/shard_map/dot_general | solution.py:85
  223.3 3.3 multiply_reduce_fusion
  227.3 2.0 fusion.20
  231.1 1.9 fusion.62
  233.0 1.9 fusion.24
  234.9 2.1 fusion.64
  237.0 1.8 fusion.6
  238.9 3.5 fusion.22
  244.4 3.3 collective-permute-start.1
  250.9 16.8 %collective-permute-done.1 = f32[512,512]{1,0:T(8,128)S(1)} collective-permute-done((f32[512,512]{1,0:T(8,128)S(1)}, f32[512,512]{1,0:T(8,128)S(1)}, u32[]{:S(2)}, u32[]{:S(2)}) %collective-permute-start.1) | collective-permute-done | bytes 1048608 | tf_op jit(solution)/shard_map/ppermute | solution.py:18
  267.6 2.5 fusion.16
  270.2 2.5 select_reduce_fusion
  272.7 13.9 %all-reduce.1 = (f32[512]{0:T(512)S(1)}, f32[512]{0:T(512)S(1)}) all-reduce(f32[512]{0:T(512)S(1)} %get-tuple-element.3, f32[512]{0:T(512)S(1)} %get-tuple-element.20), channel_id=1, replica_groups=mesh['dp_0'=8,'dp_1'=4,'mp_0'=8,'mp_1'=2] {'dp_0'}, use_global_device_ids=true, to_apply=%region_3.4 | all-reduce | flops 1024 | bytes 8192 | tf_op jit(solution)/shard_map/psum | solution.py:23
  286.6 8.7 %all-reduce.2 = (f32[512]{0:T(512)S(1)}, f32[512]{0:T(512)S(1)}) all-reduce(f32[512]{0:T(512)S(1)} %get-tuple-element.7, f32[512]{0:T(512)S(1)} %get-tuple-element.8), channel_id=1, replica_groups=mesh['dp_0'=8,'dp_1'=4,'mp_0'=8,'mp_1'=2] {'dp_1'}, use_global_device_ids=true, to_apply=%region_4.5 | all-reduce | flops 1024 | bytes 8192 | tf_op jit(solution)/shard_map/psum | solution.py:23
  295.3 13.8 %all-reduce = (f32[512]{0:T(512)S(1)}, f32[512]{0:T(512)S(1)}) all-reduce(f32[512]{0:T(512)S(1)} %get-tuple-element.9, f32[512]{0:T(512)S(1)} %get-tuple-element.10), channel_id=1, replica_groups=mesh['dp_0'=8,'dp_1'=4,'mp_0'=8,'mp_1'=2] {'mp_0'}, use_global_device_ids=true, to_apply=%region_5.6 | all-reduce | flops 1024 | bytes 8192 | tf_op jit(solution)/shard_map/psum | solution.py:23
  309.1 14.7 %all-reduce.3 = (f32[512]{0:T(512)S(1)}, f32[512]{0:T(512)S(1)}) all-reduce(f32[512]{0:T(512)S(1)} %get-tuple-element.5, f32[512]{0:T(512)S(1)} %get-tuple-element.6), channel_id=1, replica_groups=mesh['dp_0'=8,'dp_1'=4,'mp_0'=8,'mp_1'=2] {'mp_1'}, use_global_device_ids=true, to_apply=%region_6.7 | all-reduce | flops 1024 | bytes 8192 | tf_op jit(solution)/shard_map/psum | solution.py:23
  327.7 98.1 %all_to_all.21 = bf16[32,128,512]{2,1,0:T(8,128)(2,1)S(1)} all-to-all(bf16[32,128,512]{2,1,0:T(8,128)(2,1)S(1)} %constant_dynamic-update-slice_fusion), channel_id=1, replica_groups=mesh['dp_0'=8,'dp_1'=4,'mp_0'=8,'mp_1'=2] {'dp_0','dp_1'}, dimensions={0} | all-to-all | bytes 8388608 | tf_op jit(solution)/shard_map/all_to_all | solution.py:105
  425.8 2.4 fusion.12
  (31 shorter events, 15.4 us)
Async XLA Ops:
  0.6 4.4 %copy-start.3 = (bf16[128,1024]{1,0:T(8,128)(2,1)S(1)}, bf16[128,1024]{1,0:T(8,128)(2,1)}, u32[]{:S(2)}) copy-start(bf16[128,1024]{1,0:T(8,128)(2,1)} %param.4) | copy-start | bytes 786436
  122.0 92.2 %collective-permute-start = (bf16[4096,512]{1,0:T(8,128)(2,1)}, bf16[4096,512]{1,0:T(8,128)(2,1)}, u32[]{:S(2)}, u32[]{:S(2)}) collective-permute-start(bf16[4096,512]{1,0:T(8,128)(2,1)} %bitcast.10), channel_id=1, source_target_pairs={{0,16},{16,0},{32,48},{48,32},{64,80},{80,64},{96,112},{112,96},{1... | collective-permute-start | bytes 12582920 | tf_op jit(solution)/shard_map/ppermute | solution.py:18
  226.6 4.5 %copy-start.2 = (f32[512,512]{1,0:T(8,128)}, f32[512,512]{1,0:T(8,128)S(1)}, u32[]{:S(2)}) copy-start(f32[512,512]{1,0:T(8,128)S(1)} %get-tuple-element.19) | copy-start | bytes 3145732
  233.0 4.0 copy-start.1
  244.3 28.4 %copy-start = (f32[512,512]{1,0:T(8,128)}, f32[512,512]{1,0:T(8,128)S(1)}, u32[]{:S(2)}) copy-start(f32[512,512]{1,0:T(8,128)S(1)} %fusion.65) | copy-start | bytes 3145732
  244.4 23.3 %collective-permute-start.1 = (f32[512,512]{1,0:T(8,128)S(1)}, f32[512,512]{1,0:T(8,128)S(1)}, u32[]{:S(2)}, u32[]{:S(2)}) collective-permute-start(f32[512,512]{1,0:T(8,128)S(1)} %fusion.65), channel_id=1, source_target_pairs={{0,16},{16,0},{32,48},{48,32},{64,80},{80,64},{96,112},{112,96},{1... | collective-permute-start | bytes 3145736 | tf_op jit(solution)/shard_map/ppermute | solution.py:18
where the time goes:
time: 432 us; the launch traced here: 430 us
  blocking collectives  256 us (59%)
  waiting for transfers between devices  104 us (24%)
  matrix products  34.2 us (8%)
  local copies, waits for them, and re-layouts  10.8 us (2%)
  other arithmetic  10.3 us (2%)
  between operations  7.38 us (2%)
  starting transfers between devices  7.17 us (2%)
    all_to_all x1, blocking collectives, on_device(): lax.all_to_all(mixed, DP, split_axis=1, concat_axis=0, tiled=True)[:, 0, :]  107 us
    ppermute x2, waiting for transfers between devices, partner_2(): lax.ppermute(value, axis, [(i, i ^ 1 << bit) for i in range(lax.axis_size...  104 us
    all_to_all x1, blocking collectives, on_device(): lax.all_to_all(outgoing, DP, split_axis=0, concat_axis=0, tiled=True)  98.1 us
    psum x4, blocking collectives, one_axis_at_a_time(): value = lax.psum(value, axis)  51.1 us
    dot_general x11, matrix products, product(): jnp.dot(left, right, precision=lax.Precision.HIGHEST, preferred_element_t...  25.3 us
  transfers between devices with their start and end apart: 2, of which 2 were waited for; matrix products, arithmetic and copies ran while one was open for 0% of the time, Pallas kernels for 0%

commit v1 on v0

v1 whole, which is shorter than its diff:
```python
import functools

import jax
import jax.numpy as jnp
from jax import lax
from jax.experimental import pallas as pl
from jax.experimental.pallas import tpu as pltpu
from jax.sharding import Mesh
from jax.sharding import PartitionSpec as P

B = 512
CB = 2
NZ, NX, NY = 8, 4, 8
T = 128
TY = T // NY
MESH_ID = pl.DeviceIdType.MESH
f32, bf16 = jnp.float32, jnp.bfloat16


def gradient_kernel(
    act, cot, g_out, abuf, cbuf, amine, cmine, psend, precv,
    ld_sem, c1_s, c1_r, a1_s, a1_r, a2_s, a2_r, cr_s, cr_r, ar_s, ar_r, p_s, p_r,
):
    z, x, y, c = (lax.axis_index(n) for n in ("z", "x", "y", "c"))
    active = x // 2 == c
    xs = x % 2

    load_c = pltpu.make_async_copy(cot, cmine, ld_sem.at[0])
    load_a = pltpu.make_async_copy(act.at[pl.ds(pl.multiple_of(y * TY, TY), TY), :], amine, ld_sem.at[1])
    load_c.start()
    load_a.start()

    @pl.when(active)
    def _():
        for h in range(2):
            @pl.when(xs == h)
            def _():
                pltpu.make_async_copy(
                    cot.at[:, h * B : (h + 1) * B], cbuf.at[z, xs], c1_r.at[xs]
                ).start()
        pltpu.make_async_copy(
            act.at[pl.ds(pl.multiple_of(y * TY, TY), TY), pl.ds(pl.multiple_of(z * B, B), B)],
            abuf.at[z, xs, y],
            a1_r.at[0],
        ).start()

    bar = pltpu.get_barrier_semaphore()

    def hello(*dev):
        pl.semaphore_signal(bar, inc=1, device_id=dev, device_id_type=MESH_ID)

    for d in range(1, NZ):
        hello((z + d) % NZ, x, y, c)
    for d in range(1, 2 * NX):
        g = (x * 2 + c + d) % (2 * NX)
        hello(z, g // 2, y, g % 2)
    hello(z, x, (y + 1) % NY, c)
    hello(z, x, (y + NY - 1) % NY, c)
    pl.semaphore_wait(bar, NZ - 1 + 2 * NX - 1 + 2)

    load_c.wait()
    load_a.wait()

    def remote(src, dst, s, r, dev):
        return pltpu.make_async_remote_copy(
            src_ref=src, dst_ref=dst, send_sem=s, recv_sem=r, device_id=dev, device_id_type=MESH_ID
        )

    def c1(h):
        return remote(
            cmine.at[:, h * B : (h + 1) * B], cbuf.at[z, xs], c1_s.at[h], c1_r.at[xs], (z, 2 * c + h, y, x // 2)
        )

    for h in range(2):
        @pl.when(2 * c + h != x)
        def _():
            c1(h).start()

    def a1(d):
        zd = (z + d) % NZ
        return remote(
            amine.at[:, pl.ds(pl.multiple_of(zd * B, B), B)], abuf.at[z, xs, y], a1_s.at[d], a1_r.at[d], (zd, x, y, c)
        )

    @pl.when(active)
    def _():
        for d in (4, 3, 5, 2, 6, 1, 7):
            a1(d).start()

    def piece_c(k, o):
        return cbuf.at[k, o]

    def piece_a(k, o):
        return abuf.at[:, (xs + o) % 2, k]

    def ring(piece, pos, n, s_sem, r_sem, dev_of):
        def send(step, o, direction):
            chunk = (pos + n - direction * (step - 1)) % n
            i = (step - 1) * 4 + o * 2 + (direction > 0)
            ref = piece(chunk, o)
            return remote(ref, ref, s_sem.at[i], r_sem.at[i], dev_of((pos + n + direction) % n))

        def arrive(step, o, direction):
            chunk = (pos + n - direction * step) % n
            i = (step - 1) * 4 + o * 2 + (direction > 0)
            ref = piece(chunk, o)
            remote(ref, ref, s_sem.at[i], r_sem.at[i], dev_of((pos + n + direction) % n)).wait_recv()

        return send, arrive

    c_send, c_arrive = ring(piece_c, z, NZ, cr_s, cr_r, lambda k: (k, x, y, c))
    a_send, a_arrive = ring(piece_a, y, NY, ar_s, ar_r, lambda k: (z, x, k, c))
    half = NZ // 2
    moves = [(s, o, d) for s in range(1, half) for o in range(2) for d in (1, -1)] + [(half, 0, 1), (half, 1, -1)]

    for o in range(2):
        c1_wait = remote(cbuf.at[z, o], cbuf.at[z, o], c1_s.at[0], c1_r.at[o], (z, x, y, c))
        c1_wait.wait_recv()
        for d in (1, -1):
            c_send(1, o, d).start()

    def a2(d):
        ref = abuf.at[:, xs, y]
        return remote(ref, ref, a2_s.at[d], a2_r.at[xs], (z, (x + d) % NX, y, c))

    @pl.when(active)
    def _():
        for d in range(NZ):
            ref = abuf.at[(z + NZ - d) % NZ, xs, y]
            remote(ref, ref, a1_s.at[0], a1_r.at[d], (z, x, y, c)).wait_recv()
        for d in (2, 1, 3):
            a2(d).start()

    def a2_wait(s):
        @pl.when(2 * c + s != x)
        def _():
            ref = abuf.at[:, s, y]
            remote(ref, ref, a2_s.at[0], a2_r.at[s], (z, x, y, c)).wait_recv()

    for o in range(2):
        s = (xs + o) % 2
        a2_wait(s)
        for d in (1, -1):
            a_send(1, o, d).start()

    for step in range(2, half + 2):
        for o in range(2):
            for send, arrive in ((c_send, c_arrive), (a_send, a_arrive)):
                for d in (1, -1):
                    if (step - 1, o, d) in moves:
                        arrive(step - 1, o, d)
                    if (step, o, d) in moves:
                        send(step, o, d).start()

    def pcopy(r):
        return remote(psend.at[r], precv.at[r], p_s.at[r], p_r.at[r], (z, x, y, 1 - c))

    rows = B // 4
    cot_all = cbuf[...].reshape(NZ * 2 * T, B)
    for r in range(4):
        lhs = abuf[:, :, :, :, r * rows : (r + 1) * rows].reshape(NZ * 2 * T, rows)
        part = lax.dot_general(lhs, cot_all, (((0,), (0,)), ((), ())), preferred_element_type=f32)
        psend[r] = part * (1.0 / 64.0)
        if r:
            pcopy(r - 1).start()
    pcopy(3).start()

    for h in range(2):
        @pl.when(2 * c + h != x)
        def _():
            c1(h).wait_send()

    @pl.when(active)
    def _():
        for d in range(1, NZ):
            a1(d).wait_send()
        for d in range(1, NX):
            a2(d).wait_send()

    for m in moves:
        c_send(*m).wait_send()
        a_send(*m).wait_send()
    for r in range(4):
        pcopy(r).wait_recv()
        g_out[r * rows : (r + 1) * rows, :] = psend[r] + precv[r]
    for r in range(4):
        pcopy(r).wait_send()


def gradient(act, cot):
    dma = pltpu.SemaphoreType.DMA
    return pl.pallas_call(
        gradient_kernel,
        out_shape=jax.ShapeDtypeStruct((B, B), f32),
        in_specs=[pl.BlockSpec(memory_space=pl.ANY)] * 2,
        out_specs=pl.BlockSpec(memory_space=pltpu.VMEM),
        scratch_shapes=[
            pltpu.VMEM((NZ, 2, NY, TY, B), bf16),
            pltpu.VMEM((NZ, 2, T, B), bf16),
            pltpu.VMEM((TY, NZ * B), bf16),
            pltpu.VMEM((T, CB * B), bf16),
            pltpu.VMEM((4, B // 4, B), f32),
            pltpu.VMEM((4, B // 4, B), f32),
            dma((2,)),
            dma((2,)), dma((2,)),
            dma((NZ,)), dma((NZ,)),
            dma((NX,)), dma((2,)),
            dma((16,)), dma((16,)),
            dma((16,)), dma((16,)),
            dma((4,)), dma((4,)),
        ],
        compiler_params=pltpu.CompilerParams(collective_id=0, has_side_effects=True, vmem_limit_bytes=40 * 2**20),
        name="gradient",
    )(act, cot)


def split(v):
    hi = v.astype(bf16)
    return hi, (v - hi.astype(f32)).astype(bf16)


def dot3(a, b, dims=(((1,), (0,)), ((), ()))):
    def d(p, q):
        return lax.dot_general(p, q, dims, preferred_element_type=f32)

    return d(a[0], b[0]) + (d(a[0], b[1]) + d(a[1], b[0]))


SCALE0 = 1.25**3


def root_kernel(g_ref, d_ref, s_ref, w_ref, v_ref, n_ref, m_ref, r_ref):
    c = lax.axis_index("c")

    def save(ref, v):
        ref[...] = v

    g = g_ref[...]
    ridge = 0.1 * (jnp.sum(g * g, keepdims=True) / B + 1.0)
    eye = (
        lax.broadcasted_iota(jnp.int32, (B, B), 0) == lax.broadcasted_iota(jnp.int32, (B, B), 1)
    )

    @pl.when(c == 0)
    def _():
        gg = split(g_ref[...])
        w_ref[...] = dot3(gg, gg, (((1,), (1,)), ((), ())))

    @pl.when(c == 1)
    def _():
        gg = split(g_ref[...])
        w_ref[...] = dot3(gg, gg, (((0,), (0,)), ((), ())))

    stat = w_ref[...] + jnp.where(eye, ridge, 0.0)
    w_ref[...] = stat
    mag = jnp.sqrt(jnp.sum(stat * stat, keepdims=True))
    s_ref[...] = jnp.broadcast_to(SCALE0 * lax.rsqrt(jnp.sqrt(mag)), s_ref.shape)
    n_ref[...] = w_ref[...] * (0.2 / mag)

    def advance(src, dst):
        n = split(src[...])
        w_ref[...] = dot3(n, n)
        v_ref[...] = dot3(n, split(w_ref[...]))
        u = src[...] - 2.0 * w_ref[...] + v_ref[...]
        v_ref[...] = u
        left = split(w_ref[...] - 2.0 * src[...])
        dst[...] = (1.25**4) * (v_ref[...] + dot3(left, split(v_ref[...])))

    advance(n_ref, m_ref)
    r_ref[...] = n_ref[...] + m_ref[...] - dot3(split(n_ref[...]), split(m_ref[...]))
    advance(m_ref, n_ref)
    d_ref[...] = r_ref[...] + n_ref[...] - dot3(split(r_ref[...]), split(n_ref[...]))


def roots(g):
    return pl.pallas_call(
        root_kernel,
        out_shape=(jax.ShapeDtypeStruct((B, B), f32), jax.ShapeDtypeStruct((8, 128), f32)),
        in_specs=[pl.BlockSpec(memory_space=pltpu.VMEM)],
        out_specs=(pl.BlockSpec(memory_space=pltpu.VMEM),) * 2,
        scratch_shapes=[pltpu.VMEM((B, B), f32)] * 5,
        compiler_params=pltpu.CompilerParams(vmem_limit_bytes=40 * 2**20),
        name="roots",
    )(g)


def product(left, right):
    return jnp.dot(left, right, precision=lax.Precision.HIGHEST, preferred_element_type=f32)


def on_device(act, cot, owners):
    z, x, y, c = (lax.axis_index(n) for n in ("z", "x", "y", "c"))
    g = gradient(act, cot)
    dev, scale = roots(g)
    scale = scale[0, 0]
    eye = jnp.eye(B, dtype=f32)
    q = scale * (eye - dev)
    other = lax.ppermute(q, "c", [(0, 1), (1, 0)])
    left = jnp.where(c == 0, q, other)
    right = jnp.where(c == 0, other, q)
    p = product(left, product(g, right))
    sums = jnp.stack([jnp.sum(g * g, axis=0), jnp.sum(p * p, axis=0)])
    for axis in ("x", "y", "z"):
        sums = lax.psum(sums, axis)
    total = jnp.sum(sums, axis=1)
    graft = jnp.sqrt(total[0] / jnp.maximum(total[1], 1.0))
    out = (graft * p).astype(bf16).reshape(NX, B // NX, B)
    got = lax.all_to_all(out, "x", split_axis=0, concat_axis=0, tiled=True)
    update = jnp.where(c == 0, got[:2], got[2:]).transpose(1, 0, 2).reshape(B // NX, CB * B)

    s0 = scale.astype(bf16)
    s1 = (scale - s0.astype(f32)).astype(bf16)
    s2 = (scale - s0.astype(f32) - s1.astype(f32)).astype(bf16)
    lane = jnp.arange(128)
    extra = jnp.where(lane == 0, s0, jnp.where(lane == 1, s1, jnp.where(lane == 2, s2, jnp.zeros((), bf16))))
    msg = jnp.concatenate([dev.astype(bf16), jnp.broadcast_to(extra[None, :], (B, 128))], axis=1)
    perm = []
    for xx in range(NX):
        for cc in range(2):
            perm.append((xx * 2 + cc, (2 * cc + xx % 2) * 2 + xx // 2))
    msg = lax.ppermute(msg, ("x", "c"), perm)
    msg = lax.all_to_all(msg.reshape(32, 16, 640), ("z", "x"), split_axis=0, concat_axis=0, tiled=True)
    dest = jnp.arange(32, dtype=jnp.int32)
    partner = owners + 1 - 2 * (owners % 2)
    left_match = owners[None, :] == dest[:, None]
    right_match = partner[None, :] == dest[:, None]
    ids = jnp.arange(owners.shape[0], dtype=jnp.int32)
    b = jnp.sum(jnp.where(left_match | right_match, ids[None, :], 0), axis=1)
    side = jnp.where(jnp.any(left_match, axis=1), 0, 1)
    src = (b // 2) * 4 + 2 * side + b % 2
    msg = lax.all_to_all(jnp.take(msg, src, axis=0), ("z", "x"), split_axis=0, concat_axis=0, tiled=True)
    msg = msg.reshape(B, 640)
    mine = jnp.sum(msg[0, B : B + 3].astype(f32))
    root = mine * (eye - msg[:, :B].astype(f32))
    return update, root, graft


def solution(mesh):
    finer = Mesh(mesh.devices.reshape(NZ, NX, NY, 2), ("z", "x", "y", "c"))
    dp, mp = ("z", "x"), ("y", "c")
    return jax.shard_map(
        on_device,
        mesh=finer,
        in_specs=(P(dp, None), P(dp, mp), P()),
        out_specs=(P(dp, mp), P(dp, mp), P()),
        check_vma=False,
    )
```

time: 432 us -> 180 us (0.42)
  the two profiles are of different devices: /device:TPU:1 before, /device:TPU:2 now
where the time goes in v1:
time: 180 us; the launch traced here: 179 us
  Pallas kernels  56.2 us (31%)
  blocking collectives  42.2 us (23%)
  starting transfers between devices  39.4 us (22%)
  waiting for transfers between devices  18.4 us (10%)
  other arithmetic  8.55 us (5%)
  local copies, waits for them, and re-layouts  5.76 us (3%)
  between operations  4.54 us (3%)
  matrix products  3.76 us (2%)
    pallas_call x1, Pallas kernels, gradient(): pl.pallas_call(gradient_kernel, out_shape=jax.ShapeDtypeStruct((B, B), f3...  46.9 us
    psum x3, blocking collectives, on_device(): sums = lax.psum(sums, axis)  42.2 us
    all_to_all x1, starting transfers between devices, on_device(): lax.all_to_all(msg.reshape(32, 16, 640), ('z', 'x'), split_axis=0, concat...  16.1 us
    all_to_all x1, waiting for transfers between devices, on_device(): lax.all_to_all(jnp.take(msg, src, axis=0), ('z', 'x'), split_axis=0, conc...  13.3 us
    pallas_call x1, Pallas kernels, roots(): pl.pallas_call(root_kernel, out_shape=(jax.ShapeDtypeStruct((B, B), f32),...  9.28 us
    all_to_all x1, starting transfers between devices, on_device(): lax.all_to_all(jnp.take(msg, src, axis=0), ('z', 'x'), split_axis=0, conc...  8.41 us
    ppermute x1, starting transfers between devices, on_device(): msg = lax.ppermute(msg, ('x', 'c'), perm)  6.51 us
    all_to_all x1, starting transfers between devices, on_device(): got = lax.all_to_all(out, 'x', split_axis=0, concat_axis=0, tiled=True)  5.87 us
  transfers between devices with their start and end apart: 5, of which 2 were waited for; matrix products, arithmetic and copies ran while one was open for 6% of the time, Pallas kernels for 0%

profile of v1, /device:TPU:2, one launch (start us, length us, event | category | flops | bytes accessed | tf_op | source)
XLA Modules:
  0.0 178.8 jit_solution(3747909715259246795)
XLA Ops:
  0.6 1.2 copy-done
  1.9 0.9 copy-done.1
  2.8 46.9 %gradient.1.g_ref = f32[512,512]{1,0:T(8,128)S(1)} custom-call(bf16[128,4096]{1,0:T(8,128)(2,1)S(1)} %copy-done, bf16[128,1024]{1,0:T(8,128)(2,1)S(1)} %copy-done.1), custom_call_target="tpu_custom_call" | custom-call | tf_op jit(solution)/shard_map/gradient/pallas_call | solution.py:192
  49.8 9.3 %roots.1 = (f32[512,512]{1,0:T(8,128)S(1)}, f32[8,128]{1,0:T(8,128)S(1)}) custom-call(f32[512,512]{1,0:T(8,128)S(1)} %gradient.1.g_ref), custom_call_target="tpu_custom_call" | custom-call | tf_op jit(solution)/shard_map/roots/pallas_call | solution.py:276
  59.6 1.6 fusion.18
  61.2 2.4 %collective-permute-start = (f32[512,512]{1,0:T(8,128)S(1)}, f32[512,512]{1,0:T(8,128)S(1)}, u32[]{:S(2)}, u32[]{:S(2)}) collective-permute-start(f32[512,512]{1,0:T(8,128)S(1)} %get-tuple-element.8), channel_id=1, source_target_pairs={{0,1},{1,0},{2,3},{3,2},{4,5},{5,4},{6,7},{7,6},{8,9},{9,8},{10,11... | collective-permute-start | bytes 3145736 | tf_op jit(solution)/shard_map/ppermute | solution.py:298
  65.0 2.0 %pad_maximum_fusion = bf16[512,640]{1,0:T(8,128)(2,1)} fusion(bf16[512,512]{1,0:T(8,128)(2,1)} %get-tuple-element.7, bf16[640]{0:T(1024)(128)(2,1)S(1)} %pad.1.clone), kind=kLoop, calls=%fused_computation.13 | loop fusion | flops 1310720 | bytes 1180928 | tf_op jit(solution)/shard_map/concatenate | solution.py:316
  67.0 6.5 %collective-permute-start.1 = (bf16[512,640]{1,0:T(8,128)(2,1)}, bf16[512,640]{1,0:T(8,128)(2,1)}, u32[]{:S(2)}, u32[]{:S(2)}) collective-permute-start(bf16[512,640]{1,0:T(8,128)(2,1)} %pad_maximum_fusion), channel_id=1, source_target_pairs={{0,0},{1,32},{16,16},{17,48},{32,1},{33,33},{48,17},{49,49},{2,2},... | collective-permute-start | bytes 1966088 | tf_op jit(solution)/shard_map/ppermute | solution.py:321
  73.7 16.1 %all-to-all-start.1 = ((bf16[32,16,640]{2,1,0:T(8,128)(2,1)}), bf16[32,16,640]{2,1,0:T(8,128)(2,1)}, u32[]{:S(2)}, u32[]{:S(2)}) async-start(bf16[32,16,640]{2,1,0:T(8,128)(2,1)} %bitcast.6), calls=%async_computation.1 | async-start | bytes 1310720 | tf_op jit(solution)/shard_map/all_to_all | solution.py:322
  89.9 1.9 %fusion.2 = f32[512,512]{1,0:T(8,128)S(1)} fusion(f32[512,512]{1,0:T(8,128)S(1)} %gradient.1.g_ref, f32[512,512]{1,0:T(8,128)S(1)} %collective-permute-done, f32[512,512]{1,0:T(8,128)S(1)} %get-tuple-element.8, pred[]{:T(512)S(6)} %eq.70), kind=kOutput, calls=%fused_computation.7 | convolution fusion | flops 1610874880 | bytes 4194305 | tf_op jit(solution)/shard_map/dot_general | solution.py:288
  91.8 1.9 %multiply_reduce_fusion = (f32[512]{0:T(512)S(1)}, f32[512,512]{1,0:T(8,128)S(1)}) fusion(f32[512,512]{1,0:T(8,128)S(1)} %fusion.2, f32[512,512]{1,0:T(8,128)S(1)} %get-tuple-element.8, f32[512,512]{1,0:T(8,128)S(1)} %collective-permute-done, pred[]{:T(512)S(6)} %eq.70), kind=kOutput, calls=%fused_computation.6 | convolution fusion | flops 1611398656 | bytes 4196353 | tf_op jit(solution)/shard_map/dot_general | solution.py:288
  93.7 8.6 %psum.21 = f32[2,512]{1,0:T(2,128)S(1)} all-reduce(f32[2,512]{1,0:T(2,128)S(1)} %pad_maximum_fusion.1), channel_id=1, replica_groups=mesh['z'=8,'x'=4,'y'=8,'c'=2] {'x'}, use_global_device_ids=true, to_apply=%region_2.3 | all-reduce | flops 1024 | bytes 8192 | tf_op jit(solution)/shard_map/psum | solution.py:304
  102.3 16.9 %psum.22 = f32[2,512]{1,0:T(2,128)S(1)} all-reduce(f32[2,512]{1,0:T(2,128)S(1)} %psum.21), channel_id=1, replica_groups=mesh['z'=8,'x'=4,'y'=8,'c'=2] {'y'}, use_global_device_ids=true, to_apply=%region_3.4 | all-reduce | flops 1024 | bytes 8192 | tf_op jit(solution)/shard_map/psum | solution.py:304
  119.3 16.6 %psum.23 = f32[2,512]{1,0:T(2,128)S(1)} all-reduce(f32[2,512]{1,0:T(2,128)S(1)} %psum.22), channel_id=1, replica_groups=mesh['z'=8,'x'=4,'y'=8,'c'=2] {'z'}, use_global_device_ids=true, to_apply=%region_4.5 | all-reduce | flops 1024 | bytes 8192 | tf_op jit(solution)/shard_map/psum | solution.py:304
  138.0 0.9 multiply_convert_fusion
  138.9 5.9 %all-to-all-start = ((bf16[4,128,512]{2,1,0:T(8,128)(2,1)}), bf16[4,128,512]{2,1,0:T(8,128)(2,1)S(1)}, u32[]{:S(2)}, u32[]{:S(2)}) async-start(bf16[4,128,512]{2,1,0:T(8,128)(2,1)} %bitcast.4), calls=%async_computation | async-start | bytes 1048576 | tf_op jit(solution)/shard_map/all_to_all | solution.py:308
  144.8 1.8 gather_fusion
  146.6 1.0 broadcast_select_fusion
  147.5 5.2 %all-to-all-done = bf16[4,128,512]{2,1,0:T(8,128)(2,1)S(1)} async-done(((bf16[4,128,512]{2,1,0:T(8,128)(2,1)}), bf16[4,128,512]{2,1,0:T(8,128)(2,1)S(1)}, u32[]{:S(2)}, u32[]{:S(2)}) %all-to-all-start) | async-done | bytes 524320 | tf_op jit(solution)/shard_map/all_to_all | solution.py:308
  152.7 8.4 %all-to-all-start.2 = ((bf16[32,16,640]{2,1,0:T(8,128)(2,1)}), bf16[32,16,640]{2,1,0:T(8,128)(2,1)S(1)}, u32[]{:S(2)}, u32[]{:S(2)}) async-start(bf16[32,16,640]{2,1,0:T(8,128)(2,1)} %broadcast_select_fusion), calls=%async_computation.2 | async-start | bytes 1310720 | tf_op jit(solution)/shard_map/all_to_all | solution.py:331
  161.2 0.7 copy.8
  161.9 13.3 %all-to-all-done.2 = bf16[32,16,640]{2,1,0:T(8,128)(2,1)S(1)} async-done(((bf16[32,16,640]{2,1,0:T(8,128)(2,1)}), bf16[32,16,640]{2,1,0:T(8,128)(2,1)S(1)}, u32[]{:S(2)}, u32[]{:S(2)}) %all-to-all-start.2) | async-done | bytes 655392 | tf_op jit(solution)/shard_map/all_to_all | solution.py:331
  175.2 0.7 fusion.17
  175.8 1.8 %fusion.1 = f32[512,512]{1,0:T(8,128)} fusion(bf16[512,640]{1,0:T(8,128)(2,1)S(1)} %bitcast.37, f32[]{:T(128)} %fusion.17), kind=kLoop, calls=%fused_computation.4 | loop fusion | flops 1310720 | bytes 1572868 | tf_op jit(solution)/shard_map/mul | solution.py:334
  (21 shorter events, 1.6 us)
Async XLA Ops:
  0.6 1.2 copy-start
  1.9 0.9 copy-start.1
  61.2 12.3 %copy-start.2 = (s32[16]{0:T(128)S(1)}, s32[16]{0:T(128)}, u32[]{:S(2)}) copy-start(s32[16]{0:T(128)} %param.5) | copy-start | bytes 196
  61.2 28.8 %collective-permute-start = (f32[512,512]{1,0:T(8,128)S(1)}, f32[512,512]{1,0:T(8,128)S(1)}, u32[]{:S(2)}, u32[]{:S(2)}) collective-permute-start(f32[512,512]{1,0:T(8,128)S(1)} %get-tuple-element.8), channel_id=1, source_target_pairs={{0,1},{1,0},{2,3},{3,2},{4,5},{5,4},{6,7},{7,6},{8,9},{9,8},{10,11... | collective-permute-start | bytes 3145736 | tf_op jit(solution)/shard_map/ppermute | solution.py:298
  67.0 6.7 %collective-permute-start.1 = (bf16[512,640]{1,0:T(8,128)(2,1)}, bf16[512,640]{1,0:T(8,128)(2,1)}, u32[]{:S(2)}, u32[]{:S(2)}) collective-permute-start(bf16[512,640]{1,0:T(8,128)(2,1)} %pad_maximum_fusion), channel_id=1, source_target_pairs={{0,0},{1,32},{16,16},{17,48},{32,1},{33,33},{48,17},{49,49},{2,2},... | collective-permute-start | bytes 1966088 | tf_op jit(solution)/shard_map/ppermute | solution.py:321
  73.7 65.2 %all-to-all-start.1 = ((bf16[32,16,640]{2,1,0:T(8,128)(2,1)}), bf16[32,16,640]{2,1,0:T(8,128)(2,1)}, u32[]{:S(2)}, u32[]{:S(2)}) async-start(bf16[32,16,640]{2,1,0:T(8,128)(2,1)} %bitcast.6), calls=%async_computation.1 | async-start | bytes 1310720 | tf_op jit(solution)/shard_map/all_to_all | solution.py:322
  138.9 13.8 %all-to-all-start = ((bf16[4,128,512]{2,1,0:T(8,128)(2,1)}), bf16[4,128,512]{2,1,0:T(8,128)(2,1)S(1)}, u32[]{:S(2)}, u32[]{:S(2)}) async-start(bf16[4,128,512]{2,1,0:T(8,128)(2,1)} %bitcast.4), calls=%async_computation | async-start | bytes 1048576 | tf_op jit(solution)/shard_map/all_to_all | solution.py:308
  152.7 22.5 %all-to-all-start.2 = ((bf16[32,16,640]{2,1,0:T(8,128)(2,1)}), bf16[32,16,640]{2,1,0:T(8,128)(2,1)S(1)}, u32[]{:S(2)}, u32[]{:S(2)}) async-start(bf16[32,16,640]{2,1,0:T(8,128)(2,1)} %broadcast_select_fusion), calls=%async_computation.2 | async-start | bytes 1310720 | tf_op jit(solution)/shard_map/all_to_all | solution.py:331

commit v2 on v1

--- a/solution.py
+++ b/solution.py
@@ -17,11 +17,21 @@
 f32, bf16 = jnp.float32, jnp.bfloat16
 
 
-def gradient_kernel(
+def remote(src, dst, s, r, dev):
+    return pltpu.make_async_remote_copy(
+        src_ref=src, dst_ref=dst, send_sem=s, recv_sem=r, device_id=dev, device_id_type=MESH_ID
+    )
+
+
+def coords():
+    return tuple(lax.axis_index(n) for n in ("z", "x", "y", "c"))
+
+
+def gradient_stage(
     act, cot, g_out, abuf, cbuf, amine, cmine, psend, precv,
     ld_sem, c1_s, c1_r, a1_s, a1_r, a2_s, a2_r, cr_s, cr_r, ar_s, ar_r, p_s, p_r,
 ):
-    z, x, y, c = (lax.axis_index(n) for n in ("z", "x", "y", "c"))
+    z, x, y, c = coords()
     active = x // 2 == c
     xs = x % 2
 
@@ -49,22 +59,15 @@
     def hello(*dev):
         pl.semaphore_signal(bar, inc=1, device_id=dev, device_id_type=MESH_ID)
 
-    for d in range(1, NZ):
-        hello((z + d) % NZ, x, y, c)
-    for d in range(1, 2 * NX):
-        g = (x * 2 + c + d) % (2 * NX)
-        hello(z, g // 2, y, g % 2)
-    hello(z, x, (y + 1) % NY, c)
-    hello(z, x, (y + NY - 1) % NY, c)
-    pl.semaphore_wait(bar, NZ - 1 + 2 * NX - 1 + 2)
+    for d in range(1, 2 * NX * NZ):
+        g = (z * 2 * NX + x * 2 + c + d) % (2 * NX * NZ)
+        hello(g // (2 * NX), g // 2 % NX, y, g % 2)
+    for d in range(1, NY):
+        hello(z, x, (y + d) % NY, c)
+    pl.semaphore_wait(bar, 2 * NX * NZ - 1 + NY - 1)
 
     load_c.wait()
     load_a.wait()
-
-    def remote(src, dst, s, r, dev):
-        return pltpu.make_async_remote_copy(
-            src_ref=src, dst_ref=dst, send_sem=s, recv_sem=r, device_id=dev, device_id_type=MESH_ID
-        )
 
     def c1(h):
         return remote(
@@ -187,33 +190,6 @@
         pcopy(r).wait_send()
 
 
-def gradient(act, cot):
-    dma = pltpu.SemaphoreType.DMA
-    return pl.pallas_call(
-        gradient_kernel,
-        out_shape=jax.ShapeDtypeStruct((B, B), f32),
-        in_specs=[pl.BlockSpec(memory_space=pl.ANY)] * 2,
-        out_specs=pl.BlockSpec(memory_space=pltpu.VMEM),
-        scratch_shapes=[
-            pltpu.VMEM((NZ, 2, NY, TY, B), bf16),
-            pltpu.VMEM((NZ, 2, T, B), bf16),
-            pltpu.VMEM((TY, NZ * B), bf16),
-            pltpu.VMEM((T, CB * B), bf16),
-            pltpu.VMEM((4, B // 4, B), f32),
-            pltpu.VMEM((4, B // 4, B), f32),
-            dma((2,)),
-            dma((2,)), dma((2,)),
-            dma((NZ,)), dma((NZ,)),
-            dma((NX,)), dma((2,)),
-            dma((16,)), dma((16,)),
-            dma((16,)), dma((16,)),
-            dma((4,)), dma((4,)),
-        ],
-        compiler_params=pltpu.CompilerParams(collective_id=0, has_side_effects=True, vmem_limit_bytes=40 * 2**20),
-        name="gradient",
-    )(act, cot)
-
-
 def split(v):
     hi = v.astype(bf16)
     return hi, (v - hi.astype(f32)).astype(bf16)
@@ -229,11 +205,8 @@
 SCALE0 = 1.25**3
 
 
-def root_kernel(g_ref, d_ref, s_ref, w_ref, v_ref, n_ref, m_ref, r_ref):
+def root_stage(g_ref, d_ref, s_ref, w_ref, v_ref, n_ref, m_ref, r_ref):
     c = lax.axis_index("c")
-
-    def save(ref, v):
-        ref[...] = v
 
     g = g_ref[...]
     ridge = 0.1 * (jnp.sum(g * g, keepdims=True) / B + 1.0)
@@ -272,67 +245,316 @@
     d_ref[...] = r_ref[...] + n_ref[...] - dot3(split(r_ref[...]), split(n_ref[...]))
 
 
-def roots(g):
+PAIRS = [(i, j) for i in range(4) for j in range(i, 4)]
+MID = 16
+PIECE = len(PAIRS) * 128 // MID
+
+
+def exchange(box, value, me, n, dev_of, s, r):
+    box[me] = value
+    for d in range(1, n):
+        remote(box.at[me], box.at[me], s.at[d], r.at[d], dev_of((me + d) % n)).start()
+
+
+def exchanged(box, me, n, dev_of, s, r):
+    for d in range(1, n):
+        ref = box.at[(me + n - d) % n]
+        remote(ref, ref, s.at[d], r.at[d], dev_of(me)).wait_recv()
+    total = box[0]
+    for i in range(1, n):
+        total = total + box[i]
+    return total
+
+
+def sent(box, me, n, dev_of, s, r):
+    for d in range(1, n):
+        remote(box.at[me], box.at[me], s.at[d], r.at[d], dev_of((me + d) % n)).wait_send()
+
+
+def finish_stage(
+    src, g, dev, scale, pbox, bbox, graft,
+    dhi, dlo, phi, plo, pscale, pack, abox, stage, t_ref, pout, box1, box2, box3,
+    d_s, d_r, a_s, a_r, b_s, b_r, o_s, o_r, e1_s, e1_r, e2_s, e2_r, e3_s, e3_r,
+):
+    z, x, y, c = coords()
+    kappa, xs = x // 2, x % 2
+    other = (z, x, y, 1 - c)
+    half = B // 2
+
+    dhi[...] = dev[...].astype(bf16)
+    dlo[...] = (dev[...] - dhi[...].astype(f32)).astype(bf16)
+
+    for n, (i, j) in enumerate(PAIRS):
+        pack[n * 128 : (n + 1) * 128, :] = dhi[i * 128 : (i + 1) * 128, j * 128 : (j + 1) * 128]
+    sv = scale[0:1, 0:1]
+    s0 = sv.astype(bf16).astype(f32)
+    s1 = (sv - s0).astype(bf16).astype(f32)
+    s2 = sv - s0 - s1
+    row = lax.broadcasted_iota(jnp.int32, (16, 128), 0)
+    col = lax.broadcasted_iota(jnp.int32, (16, 128), 1)
+    end = pack.shape[0]
+    last = pack[end - 16 : end, :].astype(f32)
+    for k, v in enumerate((s0, s1, s2)):
+        last = jnp.where((row == 15) & (col == k), v, last)
+    pack[end - 16 : end, :] = last.astype(bf16)
+
+    def cross(lo):
+        rows = pl.ds(lo, B - lo)
+        return [
+            remote(dhi.at[rows], phi.at[rows], d_s.at[0], d_r.at[0], other),
+            remote(dlo.at[rows], plo.at[rows], d_s.at[1], d_r.at[1], other),
+            remote(scale, pscale, d_s.at[2], d_r.at[2], other),
+        ]
+
+    @pl.when(c == 0)
+    def _():
+        for t in cross(half):
+            t.start()
+
+    @pl.when(c == 1)
+    def _():
+        for t in cross(0):
+            t.start()
+
+    mine = z * 4 + 2 * c + xs
+    forwards = xs == c
+    k_me = z * 2 + x // 2
+
+    def leg_a(k):
+        rows = pl.ds(pl.multiple_of(k * PIECE, 16), PIECE)
+        return remote(
+            pack.at[rows], abox.at[mine], a_s.at[k], a_r.at[mine], (k // 2, 2 * (k % 2) + kappa, y, kappa)
+        )
+
+    def is_me(k):
+        return (k == k_me) & forwards & (kappa == c)
+
+    for t in range(MID):
+        k = (t + 2 * z) % MID
+
+        @pl.when(jnp.logical_not(is_me(k)))
+        def _():
+            leg_a(k).start()
+
+    @pl.when(forwards & (kappa == c))
+    def _():
+        abox[mine] = pack[pl.ds(pl.multiple_of(k_me * PIECE, 16), PIECE), :]
+
+    @pl.when(c == 0)
+    def _():
+        u = g[:half, :] - dot3((dhi[:half, :], dlo[:half, :]), split(g[...]))
+        t_ref[:half, :] = u
+        for t in cross(0):
+            t.wait_recv()
+        factor = scale[0:1, 0:1] * pscale[0:1, 0:1]
+        for r in range(2):
+            u = t_ref[r * 128 : (r + 1) * 128, :]
+            pout[r] = factor * (u - dot3(split(u), (phi[...], plo[...])))
+
+    @pl.when(c == 1)
+    def _():
+        t_ref[...] = g[...] - dot3(split(g[...]), (dhi[...], dlo[...]))
+        for t in cross(half):
+            t.wait_recv()
+        factor = scale[0:1, 0:1] * pscale[0:1, 0:1]
+        tt = split(t_ref[...])
+        for r in range(2):
+            rows = slice(half + r * 128, half + (r + 1) * 128)
+            pout[r] = factor * (t_ref[rows, :] - dot3((phi[rows, :], plo[rows, :]), tt))
+
+    sum_p = jnp.sum(pout[...] * pout[...], axis=0)
+    sum_p = jnp.sum(sum_p, keepdims=True)
+    sum_g = 0.5 * jnp.sum(g[...] * g[...], keepdims=True)
+    row8 = lax.broadcasted_iota(jnp.int32, (8, 128), 0)
+    value = jnp.where(row8 == 0, sum_p, jnp.where(row8 == 1, sum_g, 0.0))
+
+    e1 = (box1, x * 2 + c, 2 * NX, lambda i: (z, i // 2, y, i % 2), e1_s, e1_r)
+    e2 = (box2, y, NY, lambda i: (z, x, i, c), e2_s, e2_r)
+    e3 = (box3, z, NZ, lambda i: (i, x, y, c), e3_s, e3_r)
+    exchange(e1[0], value, *e1[1:])
+
+    def rows_to(r):
+        return remote(
+            pout.at[r], pbox.at[:, pl.ds(pl.multiple_of(xs * B, B), B)], o_s.at[r], o_r.at[xs], (z, 2 * c + r, y, kappa)
+        )
+
+    for r in range(2):
+        @pl.when(2 * c + r != x)
+        def _():
+            rows_to(r).start()
+
+        @pl.when(2 * c + r == x)
+        def _():
+            pbox[:, pl.ds(pl.multiple_of(xs * B, B), B)] = pout[r]
+
+    exchange(e2[0], exchanged(*e1), *e2[1:])
+
+    def leg_b(t):
+        d = (z * NX + x + t) % (NZ * NX)
+        return remote(stage.at[t], bbox.at[k_me], b_s.at[t], b_r.at[k_me], (d // NX, d % NX, y, c))
+
+    @pl.when(forwards)
+    def _():
+        for p in range(NZ * NX):
+            @pl.when(jnp.logical_not((p == mine) & (kappa == c)))
+            def _():
+                remote(abox.at[p], abox.at[p], a_s.at[0], a_r.at[p], other).wait_recv()
+        for t in range(NZ * NX):
+            piece = abox[src[(z * NX + x + t) % (NZ * NX)]]
+            if t:
+                stage[t] = piece
+            else:
+                bbox[k_me] = piece
+        for t in range(1, NZ * NX):
+            leg_b(t).start()
+
+    exchange(e3[0], exchanged(*e2), *e3[1:])
+    total = exchanged(*e3)
+    graft[...] = jnp.broadcast_to(jnp.sqrt(total[1:2, :] / jnp.maximum(total[0:1, :], 1.0)), graft.shape)
+
+    for s in range(2):
+        @pl.when(2 * c + s != x)
+        def _():
+            ref = pbox.at[:, s * B : (s + 1) * B]
+            remote(ref, ref, o_s.at[0], o_r.at[s], other).wait_recv()
+    for k in range(MID):
+        @pl.when(jnp.logical_not((k == k_me) & forwards))
+        def _():
+            remote(bbox.at[k], bbox.at[k], b_s.at[0], b_r.at[k], other).wait_recv()
+
+    @pl.when(c == 0)
+    def _():
+        for t in cross(half):
+            t.wait_send()
+
+    @pl.when(c == 1)
+    def _():
+        for t in cross(0):
+            t.wait_send()
+
+    for k in range(MID):
+        @pl.when(jnp.logical_not(is_me(k)))
+        def _():
+            leg_a(k).wait_send()
+
+    for r in range(2):
+        @pl.when(2 * c + r != x)
+        def _():
+            rows_to(r).wait_send()
+
+    @pl.when(forwards)
+    def _():
+        for t in range(1, NZ * NX):
+            leg_b(t).wait_send()
+
+    for e in (e1, e2, e3):
+        sent(*e)
+
+
+N_GRAD = 6 + 13
+N_ROOT = 5
+
+
+def step_kernel(src, act, cot, pbox, bbox, graft, g, dev, scale, *refs):
+    grad, root, rest = refs[:N_GRAD], refs[N_GRAD : N_GRAD + N_ROOT], refs[N_GRAD + N_ROOT :]
+    gradient_stage(act, cot, g, *grad)
+    root_stage(g, dev, scale, *root)
+    finish_stage(src, g, dev, scale, pbox, bbox, graft, *rest)
+
+
+def step(src, act, cot):
+    dma = pltpu.SemaphoreType.DMA
+    vmem = pltpu.VMEM
+    in_vmem = pl.BlockSpec(memory_space=pltpu.VMEM)
     return pl.pallas_call(
-        root_kernel,
-        out_shape=(jax.ShapeDtypeStruct((B, B), f32), jax.ShapeDtypeStruct((8, 128), f32)),
-        in_specs=[pl.BlockSpec(memory_space=pltpu.VMEM)],
-        out_specs=(pl.BlockSpec(memory_space=pltpu.VMEM),) * 2,
-        scratch_shapes=[pltpu.VMEM((B, B), f32)] * 5,
-        compiler_params=pltpu.CompilerParams(vmem_limit_bytes=40 * 2**20),
-        name="roots",
-    )(g)
-
-
-def product(left, right):
-    return jnp.dot(left, right, precision=lax.Precision.HIGHEST, preferred_element_type=f32)
+        step_kernel,
+        out_shape=(
+            jax.ShapeDtypeStruct((B // NX, CB * B), f32),
+            jax.ShapeDtypeStruct((MID, PIECE, 128), bf16),
+            jax.ShapeDtypeStruct((8, 128), f32),
+        ),
+        in_specs=[
+            pl.BlockSpec(memory_space=pltpu.SMEM),
+            pl.BlockSpec(memory_space=pl.ANY),
+            pl.BlockSpec(memory_space=pl.ANY),
+        ],
+        out_specs=(in_vmem,) * 3,
+        scratch_shapes=[
+            vmem((B, B), f32), vmem((B, B), f32), vmem((8, 128), f32),
+            vmem((NZ, 2, NY, TY, B), bf16),
+            vmem((NZ, 2, T, B), bf16),
+            vmem((TY, NZ * B), bf16),
+            vmem((T, CB * B), bf16),
+            vmem((4, B // 4, B), f32),
+            vmem((4, B // 4, B), f32),
+            dma((2,)),
+            dma((2,)), dma((2,)),
+            dma((NZ,)), dma((NZ,)),
+            dma((NX,)), dma((2,)),
+            dma((16,)), dma((16,)),
+            dma((16,)), dma((16,)),
+            dma((4,)), dma((4,)),
+            *[vmem((B, B), f32)] * N_ROOT,
+            vmem((B, B), bf16), vmem((B, B), bf16), vmem((B, B), bf16), vmem((B, B), bf16),
+            vmem((8, 128), f32),
+            vmem((MID * PIECE, 128), bf16),
+            vmem((NZ * NX, PIECE, 128), bf16),
+            vmem((NZ * NX, PIECE, 128), bf16),
+            vmem((B, B), f32),
+            vmem((2, 128, B), f32),
+            vmem((8, 8, 128), f32), vmem((8, 8, 128), f32), vmem((8, 8, 128), f32),
+            dma((3,)), dma((3,)),
+            dma((MID,)), dma((NZ * NX,)),
+            dma((NZ * NX,)), dma((MID,)),
+            dma((2,)), dma((2,)),
+            dma((8,)), dma((8,)), dma((8,)), dma((8,)), dma((8,)), dma((8,)),
+        ],
+        compiler_params=pltpu.CompilerParams(
+            collective_id=0, has_side_effects=True, vmem_limit_bytes=60 * 2**20
+        ),
+        name="step",
+    )(src, act, cot)
+
+
+def output_kernel(pbox, bbox, graft, update, root):
+    update[...] = (graft[0:1, 0:1] * pbox[...]).astype(bf16)
+    corner = bbox[len(PAIRS) * 128 - 16 :, :].astype(f32)[15:16, :]
+    scale = corner[:, 0:1] + corner[:, 1:2] + corner[:, 2:3]
+    row = lax.broadcasted_iota(jnp.int32, (128, 128), 0)
+    col = lax.broadcasted_iota(jnp.int32, (128, 128), 1)
+    for n, (i, j) in enumerate(PAIRS):
+        block = bbox[n * 128 : (n + 1) * 128, :].astype(f32)
+        if i == j:
+            if i == 3:
+                block = jnp.where((row == 127) & (col < 3), block.T, block)
+            block = scale * (jnp.where(row == col, 1.0, 0.0) - block)
+        else:
+            block = -scale * block
+            root[j * 128 : (j + 1) * 128, i * 128 : (i + 1) * 128] = block.T
+        root[i * 128 : (i + 1) * 128, j * 128 : (j + 1) * 128] = block
+
+
+def outputs(pbox, bbox, graft):
+    vmem = pl.BlockSpec(memory_space=pltpu.VMEM)
+    return pl.pallas_call(
+        output_kernel,
+        out_shape=(jax.ShapeDtypeStruct((B // NX, CB * B), bf16), jax.ShapeDtypeStruct((B, B), f32)),
+        in_specs=[vmem] * 3,
+        out_specs=(vmem, vmem),
+        name="outputs",
+    )(pbox, bbox.reshape(MID * PIECE, 128), graft)
 
 
 def on_device(act, cot, owners):
-    z, x, y, c = (lax.axis_index(n) for n in ("z", "x", "y", "c"))
-    g = gradient(act, cot)
-    dev, scale = roots(g)
-    scale = scale[0, 0]
-    eye = jnp.eye(B, dtype=f32)
-    q = scale * (eye - dev)
-    other = lax.ppermute(q, "c", [(0, 1), (1, 0)])
-    left = jnp.where(c == 0, q, other)
-    right = jnp.where(c == 0, other, q)
-    p = product(left, product(g, right))
-    sums = jnp.stack([jnp.sum(g * g, axis=0), jnp.sum(p * p, axis=0)])
-    for axis in ("x", "y", "z"):
-        sums = lax.psum(sums, axis)
-    total = jnp.sum(sums, axis=1)
-    graft = jnp.sqrt(total[0] / jnp.maximum(total[1], 1.0))
-    out = (graft * p).astype(bf16).reshape(NX, B // NX, B)
-    got = lax.all_to_all(out, "x", split_axis=0, concat_axis=0, tiled=True)
-    update = jnp.where(c == 0, got[:2], got[2:]).transpose(1, 0, 2).reshape(B // NX, CB * B)
-
-    s0 = scale.astype(bf16)
-    s1 = (scale - s0.astype(f32)).astype(bf16)
-    s2 = (scale - s0.astype(f32) - s1.astype(f32)).astype(bf16)
-    lane = jnp.arange(128)
-    extra = jnp.where(lane == 0, s0, jnp.where(lane == 1, s1, jnp.where(lane == 2, s2, jnp.zeros((), bf16))))
-    msg = jnp.concatenate([dev.astype(bf16), jnp.broadcast_to(extra[None, :], (B, 128))], axis=1)
-    perm = []
-    for xx in range(NX):
-        for cc in range(2):
-            perm.append((xx * 2 + cc, (2 * cc + xx % 2) * 2 + xx // 2))
-    msg = lax.ppermute(msg, ("x", "c"), perm)
-    msg = lax.all_to_all(msg.reshape(32, 16, 640), ("z", "x"), split_axis=0, concat_axis=0, tiled=True)
-    dest = jnp.arange(32, dtype=jnp.int32)
-    partner = owners + 1 - 2 * (owners % 2)
+    dest = jnp.arange(NZ * NX, dtype=jnp.int32)
     left_match = owners[None, :] == dest[:, None]
-    right_match = partner[None, :] == dest[:, None]
+    right_match = (owners + 1 - 2 * (owners % 2))[None, :] == dest[:, None]
     ids = jnp.arange(owners.shape[0], dtype=jnp.int32)
-    b = jnp.sum(jnp.where(left_match | right_match, ids[None, :], 0), axis=1)
-    side = jnp.where(jnp.any(left_match, axis=1), 0, 1)
-    src = (b // 2) * 4 + 2 * side + b % 2
-    msg = lax.all_to_all(jnp.take(msg, src, axis=0), ("z", "x"), split_axis=0, concat_axis=0, tiled=True)
-    msg = msg.reshape(B, 640)
-    mine = jnp.sum(msg[0, B : B + 3].astype(f32))
-    root = mine * (eye - msg[:, :B].astype(f32))
-    return update, root, graft
+    place = (ids // 2) * 4 + ids % 2
+    src = jnp.sum(jnp.where(left_match, place[None, :], 0) + jnp.where(right_match, place[None, :] + 2, 0), axis=1)
+    pbox, bbox, graft = step(src, act, cot)
+    update, root = outputs(pbox, bbox, graft)
+    return update, root, graft[0, 0]
 
 
 def solution(mesh):

time: 180 us -> 95.4 us (0.53)
  the two profiles are of different devices: /device:TPU:2 before, /device:TPU:1 now
where the time goes in v2:
time: 95.4 us; the launch traced here: 93.7 us
  Pallas kernels  89.9 us (94%)
  local copies, waits for them, and re-layouts  1.83 us (2%)
  other arithmetic  1.28 us (1%)
    pallas_call x1, Pallas kernels, step(): pl.pallas_call(step_kernel, out_shape=(jax.ShapeDtypeStruct((B // NX, CB...  87.5 us
    pallas_call x1, Pallas kernels, outputs(): pl.pallas_call(output_kernel, out_shape=(jax.ShapeDtypeStruct((B // NX, C...  2.46 us

profile of v2, /device:TPU:1, one launch (start us, length us, event | category | flops | bytes accessed | tf_op | source)
XLA Modules:
  0.0 93.7 jit_solution(4879740893369445745)
XLA Ops:
  0.6 0.7 fusion
  1.3 0.0 copy-start
  1.3 0.6 copy-done
  2.0 0.6 add_reduce_fusion.src
  2.6 87.5 %step.1 = (f32[128,1024]{1,0:T(8,128)}, bf16[16,80,128]{2,1,0:T(8,128)(2,1)}, f32[8,128]{1,0:T(8,128)}) custom-call(s32[32]{0:T(128)} %add_reduce_fusion.src, bf16[128,4096]{1,0:T(8,128)(2,1)} %act.1, bf16[128,1024]{1,0:T(8,128)(2,1)} %cot.1), custom_call_target="tpu_custom_call" | custom-call | tf_op jit(solution)/shard_map/step/pallas_call | solution.py:469
  90.0 2.5 %outputs.1 = (bf16[128,1024]{1,0:T(8,128)(2,1)}, f32[512,512]{1,0:T(8,128)}) custom-call(f32[128,1024]{1,0:T(8,128)} %get-tuple-element.8.pbox, bf16[1280,128]{1,0:T(8,128)(2,1)} %bitcast.2, f32[8,128]{1,0:T(8,128)} %get-tuple-element.10.graft), custom_call_target="tpu_custom_call" | custom-call | tf_op jit(solution)/shard_map/outputs/pallas_call | solution.py:539
  92.5 1.2 %slice.3 = f32[1,1]{1,0:T(1,128)} slice(f32[8,128]{1,0:T(8,128)} %get-tuple-element.10.graft), slice={[0:1], [0:1]} | slice | bytes 8 | tf_op jit(solution)/shard_map/slice | solution.py:557
  (1 shorter events, 0.0 us)
Async XLA Ops:
  1.3 0.7 copy-start

commit v3 on v2

v3 whole, which is shorter than its diff:
```python
import functools

import jax
import jax.numpy as jnp
from jax import lax
from jax.experimental import pallas as pl
from jax.experimental.pallas import tpu as pltpu
from jax.sharding import Mesh
from jax.sharding import PartitionSpec as P

B = 512
CB = 2
NZ, NX, NY = 8, 4, 8
NB = 16
T = 128
TY = T // NY
MESH_ID = pl.DeviceIdType.MESH
f32, bf16 = jnp.float32, jnp.bfloat16


def remote(src, dst, s, r, dev):
    return pltpu.make_async_remote_copy(
        src_ref=src, dst_ref=dst, send_sem=s, recv_sem=r, device_id=dev, device_id_type=MESH_ID
    )


def coords():
    return tuple(lax.axis_index(n) for n in ("z", "x", "y", "c"))


def gradient_stage(
    act, cot, g_out, table, abuf, cbuf, amine, cmine, psend, precv,
    ld_sem, c1_s, c1_r, a1_s, a1_r, a2_s, a2_r, cr_s, cr_r, ar_s, ar_r, w_s, w_r, p_s, p_r,
):
    z, x, y, c = coords()
    active = x // 2 == c
    xs = x % 2

    load_c = pltpu.make_async_copy(cot, cmine, ld_sem.at[0])
    load_a = pltpu.make_async_copy(act.at[pl.ds(pl.multiple_of(y * TY, TY), TY), :], amine, ld_sem.at[1])
    load_c.start()
    load_a.start()

    @pl.when(active)
    def _():
        for h in range(2):
            @pl.when(xs == h)
            def _():
                pltpu.make_async_copy(
                    cot.at[:, h * B : (h + 1) * B], cbuf.at[z, xs], c1_r.at[xs]
                ).start()
        pltpu.make_async_copy(
            act.at[pl.ds(pl.multiple_of(y * TY, TY), TY), pl.ds(pl.multiple_of(z * B, B), B)],
            abuf.at[z, xs, y],
            a1_r.at[0],
        ).start()

    bar = pltpu.get_barrier_semaphore()

    def hello(*dev):
        pl.semaphore_signal(bar, inc=1, device_id=dev, device_id_type=MESH_ID)

    for d in range(1, 2 * NX * NZ):
        g = (z * 2 * NX + x * 2 + c + d) % (2 * NX * NZ)
        hello(g // (2 * NX), g // 2 % NX, y, g % 2)
    for d in range(1, NY):
        hello(z, x, (y + d) % NY, c)
    pl.semaphore_wait(bar, 2 * NX * NZ - 1 + NY - 1)

    load_c.wait()
    load_a.wait()

    def c1(h):
        return remote(
            cmine.at[:, h * B : (h + 1) * B], cbuf.at[z, xs], c1_s.at[h], c1_r.at[xs], (z, 2 * c + h, y, x // 2)
        )

    for h in range(2):
        @pl.when(2 * c + h != x)
        def _():
            c1(h).start()

    def a1(d):
        zd = (z + d) % NZ
        return remote(
            amine.at[:, pl.ds(pl.multiple_of(zd * B, B), B)], abuf.at[z, xs, y], a1_s, a1_r.at[d], (zd, x, y, c)
        )

    @pl.when(active)
    def _():
        for d in (4, 3, 5, 2, 6, 1, 7):
            a1(d).start()

    table()

    half = NZ // 2
    c_moves = [(s, o, d) for s in range(1, half) for o in range(2) for d in (1, -1)] + [(half, 0, 1), (half, 1, -1)]

    def c_move(step, o, direction, back):
        chunk = (z + NZ - direction * (step - 1 + back)) % NZ
        ref = cbuf.at[chunk, o]
        i = (step - 1) * 4 + o * 2 + (direction > 0)
        return remote(ref, ref, cr_s, cr_r.at[i], ((z + NZ + direction) % NZ, x, y, c))

    def c_step(step):
        for o in range(2):
            for d in (1, -1):
                if (step, o, d) in c_moves:
                    c_move(step, o, d, 1).wait_recv()
                if (step + 1, o, d) in c_moves:
                    c_move(step + 1, o, d, 0).start()

    offsets = (0, -1, 1, -2, 2, -3, 3, 4)
    halves = (slice(0, half), slice(half, NZ))

    def at_y(q):
        return (y + NY + offsets[q]) % NY

    def y_move(step, direction, back):
        k = (y + NY - direction * (step - 1 + back)) % NY
        part = slice(0, NZ) if step < NY // 2 else halves[direction < 0]
        ref = abuf.at[part, xs, k]
        i = (step - 1) * 2 + (direction > 0)
        return remote(ref, ref, ar_s, ar_r.at[i], (z, x, (y + NY + direction) % NY, c))

    def x_move(q, s, direction):
        ref = abuf.at[:, s, at_y(q)]
        i = q * 4 + s * 2 + (direction > 0)
        return remote(ref, ref, a2_s, a2_r.at[i], (z, (x + NX + direction) % NX, y, c))

    def x_half(q, s, direction):
        ref = abuf.at[halves[direction < 0], s, at_y(q)]
        i = q * 4 + s * 2 + (direction > 0)
        return remote(ref, ref, w_s.at[s], w_r.at[i], (z, (x + NX + direction) % NX, y, c))

    def x_start(q):
        for d in (1, -1):
            x_move(q, xs, d).start()

    def x_relay(q):
        for s in range(2):
            for d, place in ((1, 1), (-1, 3)):
                @pl.when((x + NX - 2 * c - s) % NX == place)
                def _():
                    x_move(q, s, d).wait_recv()
                    x_half(q, s, d).start()

    def y_step(step):
        @pl.when(active)
        def _():
            for d in (1, -1):
                y_move(step, d, 1).wait_recv()
                if step + 1 <= NY // 2:
                    y_move(step + 1, d, 0).start()
                if step < NY // 2:
                    x_start(2 * step - (d > 0))
            if step == NY // 2:
                x_start(NY - 1)

    for o in range(2):
        c1_wait = remote(cbuf.at[z, o], cbuf.at[z, o], c1_s.at[0], c1_r.at[o], (z, x, y, c))
        c1_wait.wait_recv()
        for d in (1, -1):
            c_move(1, o, d, 0).start()

    @pl.when(active)
    def _():
        for d in range(NZ):
            ref = abuf.at[(z + NZ - d) % NZ, xs, y]
            remote(ref, ref, a1_s, a1_r.at[d], (z, x, y, c)).wait_recv()
        for d in (1, -1):
            y_move(1, d, 0).start()
        x_start(0)

    y_step(1)
    x_relay(0)
    c_step(1)
    y_step(2)
    x_relay(1)
    x_relay(2)
    y_step(3)
    c_step(2)
    x_relay(3)
    x_relay(4)
    y_step(4)
    x_relay(5)
    x_relay(6)
    c_step(3)
    x_relay(7)
    c_step(4)
    for s in range(2):
        @pl.when((x + NX - 2 * c - s) % NX == 2)
        def _():
            for q in range(NY):
                for d in (1, -1):
                    x_half(q, s, d).wait_recv()

    def pcopy(r):
        return remote(psend.at[r], precv.at[r], p_s.at[r], p_r.at[r], (z, x, y, 1 - c))

    rows = B // 4
    cot_all = cbuf[...].reshape(NZ * 2 * T, B)
    for r in range(4):
        lhs = abuf[:, :, :, :, r * rows : (r + 1) * rows].reshape(NZ * 2 * T, rows)
        part = lax.dot_general(lhs, cot_all, (((0,), (0,)), ((), ())), preferred_element_type=f32)
        psend[r] = part * (1.0 / 64.0)
        if r:
            pcopy(r - 1).start()
    pcopy(3).start()

    for h in range(2):
        @pl.when(2 * c + h != x)
        def _():
            c1(h).wait_send()

    @pl.when(active)
    def _():
        remote(abuf.at[0:7, 0, y], abuf.at[0:7, 0, y], a1_s, a1_r.at[0], (z, x, y, c)).wait_send()
        line = abuf.at[0:7, 0]
        remote(line, line, ar_s, ar_r.at[0], (z, x, y, c)).wait_send()
        line = abuf.at[:, :, :]
        remote(line, line, a2_s, a2_r.at[0], (z, x, y, c)).wait_send()

    for s in range(2):
        @pl.when((x + NX - 2 * c - s) % 2 == 1)
        def _():
            line = abuf.at[0:half, 0]
            remote(line, line, w_s.at[s], w_r.at[0], (z, x, y, c)).wait_send()

    line = cbuf.at[0:7]
    remote(line, line, cr_s, cr_r.at[0], (z, x, y, c)).wait_send()
    for r in range(4):
        pcopy(r).wait_recv()
        g_out[r * rows : (r + 1) * rows, :] = psend[r] + precv[r]
    for r in range(4):
        pcopy(r).wait_send()


def split(v):
    hi = v.astype(bf16)
    return hi, (v - hi.astype(f32)).astype(bf16)


def dot3(a, b, dims=(((1,), (0,)), ((), ()))):
    def d(p, q):
        return lax.dot_general(p, q, dims, preferred_element_type=f32)

    return d(a[0], b[0]) + (d(a[0], b[1]) + d(a[1], b[0]))


def dot1(a, b):
    return jnp.dot(a, b, preferred_element_type=f32)


SCALE0 = 1.25**3


def statistic_stage(g_ref, s_ref, n_ref, w_ref):
    c = lax.axis_index("c")
    g = g_ref[...]
    ridge = 0.1 * (jnp.sum(g * g, keepdims=True) / B + 1.0)
    eye = lax.broadcasted_iota(jnp.int32, (B, B), 0) == lax.broadcasted_iota(jnp.int32, (B, B), 1)

    @pl.when(c == 0)
    def _():
        gg = split(g_ref[...])
        w_ref[...] = dot3(gg, gg, (((1,), (1,)), ((), ())))

    @pl.when(c == 1)
    def _():
        gg = split(g_ref[...])
        w_ref[...] = dot3(gg, gg, (((0,), (0,)), ((), ())))

    stat = w_ref[...] + jnp.where(eye, ridge, 0.0)
    w_ref[...] = stat
    mag = jnp.sqrt(jnp.sum(stat * stat, keepdims=True))
    s_ref[...] = jnp.broadcast_to(SCALE0 * lax.rsqrt(jnp.sqrt(mag)), s_ref.shape)
    n_ref[...] = w_ref[...] * (0.2 / mag)


def chain(n_ref, d_ref, w_ref, v_ref, m_ref, r_ref, parts, dot):
    def advance(src, dst):
        n = parts(src[...])
        w_ref[...] = dot(n, n)
        v_ref[...] = dot(n, parts(w_ref[...]))
        u = src[...] - 2.0 * w_ref[...] + v_ref[...]
        v_ref[...] = u
        left = parts(w_ref[...] - 2.0 * src[...])
        dst[...] = (1.25**4) * (v_ref[...] + dot(left, parts(v_ref[...])))

    advance(n_ref, m_ref)
    r_ref[...] = n_ref[...] + m_ref[...] - dot(parts(n_ref[...]), parts(m_ref[...]))
    advance(m_ref, n_ref)
    d_ref[...] = r_ref[...] + n_ref[...] - dot(parts(r_ref[...]), parts(n_ref[...]))


PAIRS = [(i, j) for i in range(4) for j in range(i, 4)]
MID = 16
PIECE = len(PAIRS) * 128 // MID


def exchange(box, value, me, n, dev_of, s, r):
    box[me] = value
    for d in range(1, n):
        remote(box.at[me], box.at[me], s, r, dev_of((me + d) % n)).start()


def exchanged(box, me, n, dev_of, s, r):
    ref = box.at[0 : n - 1]
    remote(ref, ref, s, r, dev_of(me)).wait_recv()
    total = box[0]
    for i in range(1, n):
        total = total + box[i]
    return total


def sent(box, me, n, dev_of, s, r):
    ref = box.at[0 : n - 1]
    remote(ref, ref, s, r, dev_of(me)).wait_send()


def finish_stage(
    src, g, dev, scale, root_refs, pbox, root, graft,
    bbox, dhi, dlo, phi, plo, pscale, pack, abox, stage, t_ref, pout, box1, box2, box3,
    d_s, d_r, a_s, a_r, b_s, b_r, o_s, o_r, e1_s, e1_r, e2_s, e2_r, e3_s, e3_r,
):
    z, x, y, c = coords()
    kappa, xs = x // 2, x % 2
    other = (z, x, y, 1 - c)
    half = B // 2

    n_ref, w_ref, v_ref, m_ref, r_ref = root_refs
    for n, (i, j) in enumerate(PAIRS):
        pack[n * 128 : (n + 1) * 128, :] = n_ref[i * 128 : (i + 1) * 128, j * 128 : (j + 1) * 128].astype(bf16)
    sv = scale[0:1, 0:1]
    s0 = sv.astype(bf16).astype(f32)
    s1 = (sv - s0).astype(bf16).astype(f32)
    s2 = sv - s0 - s1
    row = lax.broadcasted_iota(jnp.int32, (16, 128), 0)
    col = lax.broadcasted_iota(jnp.int32, (16, 128), 1)
    end = pack.shape[0]
    last = pack[end - 16 : end, :].astype(f32)
    for k, v in enumerate((s0, s1, s2)):
        last = jnp.where((row == 15) & (col == k), v, last)
    pack[end - 16 : end, :] = last.astype(bf16)

    mine = z * 4 + 2 * c + xs
    forwards = xs == c
    k_me = z * 2 + x // 2

    def leg_a(k):
        rows = pl.ds(pl.multiple_of(k * PIECE, 16), PIECE)
        return remote(
            pack.at[rows], abox.at[mine], a_s, a_r, (k // 2, 2 * (k % 2) + kappa, y, kappa)
        )

    def is_me(k):
        return (k == k_me) & forwards & (kappa == c)

    for t in range(MID):
        k = (t + 2 * z) % MID

        @pl.when(jnp.logical_not(is_me(k)))
        def _():
            leg_a(k).start()

    @pl.when(forwards & (kappa == c))
    def _():
        abox[mine] = pack[pl.ds(pl.multiple_of(k_me * PIECE, 16), PIECE), :]

    chain(n_ref, dev, w_ref, v_ref, m_ref, r_ref, split, dot3)
    dhi[...] = dev[...].astype(bf16)
    dlo[...] = (dev[...] - dhi[...].astype(f32)).astype(bf16)

    def cross(lo):
        rows = pl.ds(lo, B - lo)
        return [
            remote(dhi.at[rows], phi.at[rows], d_s.at[0], d_r.at[0], other),
            remote(dlo.at[rows], plo.at[rows], d_s.at[1], d_r.at[1], other),
            remote(scale, pscale, d_s.at[2], d_r.at[2], other),
        ]

    @pl.when(c == 0)
    def _():
        for t in cross(half):
            t.start()

    @pl.when(c == 1)
    def _():
        for t in cross(0):
            t.start()

    @pl.when(c == 0)
    def _():
        t_ref[:half, :] = g[:half, :] - dot3((dhi[:half, :], dlo[:half, :]), split(g[...]))

    @pl.when(c == 1)
    def _():
        t_ref[...] = g[...] - dot3(split(g[...]), (dhi[...], dlo[...]))

    def leg_b(t):
        d = (z * NX + x + t) % (NZ * NX)
        return remote(stage.at[t], bbox.at[k_me], b_s, b_r, (d // NX, d % NX, y, c))

    @pl.when(forwards)
    def _():
        for there in range(2):
            @pl.when((kappa == c) == bool(there))
            def _():
                ref = abox.at[0 : NZ * NX - there]
                remote(ref, ref, a_s, a_r, other).wait_recv()
        for t in range(NZ * NX):
            piece = abox[src[(z * NX + x + t) % (NZ * NX)]]
            if t:
                stage[t] = piece
            else:
                bbox[k_me] = piece
    @pl.when(c == 0)
    def _():
        for t in cross(0):
            t.wait_recv()
        factor = scale[0:1, 0:1] * pscale[0:1, 0:1]
        for r in range(2):
            u = t_ref[r * 128 : (r + 1) * 128, :]
            pout[r] = factor * (u - dot3(split(u), (phi[...], plo[...])))

    @pl.when(c == 1)
    def _():
        for t in cross(half):
            t.wait_recv()
        factor = scale[0:1, 0:1] * pscale[0:1, 0:1]
        tt = split(t_ref[...])
        for r in range(2):
            rows = slice(half + r * 128, half + (r + 1) * 128)
            pout[r] = factor * (t_ref[rows, :] - dot3((phi[rows, :], plo[rows, :]), tt))

    sum_p = jnp.sum(pout[...] * pout[...], axis=0)
    sum_p = jnp.sum(sum_p, keepdims=True)
    sum_g = 0.5 * jnp.sum(g[...] * g[...], keepdims=True)
    row8 = lax.broadcasted_iota(jnp.int32, (8, 128), 0)
    value = jnp.where(row8 == 0, sum_p, jnp.where(row8 == 1, sum_g, 0.0))

    e1 = (box1, x * 2 + c, 2 * NX, lambda i: (z, i // 2, y, i % 2), e1_s, e1_r)
    e2 = (box2, y, NY, lambda i: (z, x, i, c), e2_s, e2_r)
    e3 = (box3, z, NZ, lambda i: (i, x, y, c), e3_s, e3_r)
    exchange(e1[0], value, *e1[1:])

    @pl.when(forwards)
    def _():
        for t in range(1, NZ * NX):
            leg_b(t).start()


    def rows_to(r):
        return remote(
            pout.at[r], pbox.at[:, pl.ds(pl.multiple_of(xs * B, B), B)], o_s.at[r], o_r.at[xs], (z, 2 * c + r, y, kappa)
        )

    for r in range(2):
        @pl.when(2 * c + r != x)
        def _():
            rows_to(r).start()

        @pl.when(2 * c + r == x)
        def _():
            pbox[:, pl.ds(pl.multiple_of(xs * B, B), B)] = pout[r]

    exchange(e2[0], exchanged(*e1), *e2[1:])
    exchange(e3[0], exchanged(*e2), *e3[1:])

    for there in range(2):
        @pl.when(forwards == bool(there))
        def _():
            ref = bbox.at[0 : MID - there]
            remote(ref, ref, b_s, b_r, other).wait_recv()

    row = lax.broadcasted_iota(jnp.int32, (128, 128), 0)
    col = lax.broadcasted_iota(jnp.int32, (128, 128), 1)
    whole = bbox[...].reshape(MID * PIECE, 128)
    for n, (i, j) in enumerate(PAIRS):
        block = whole[n * 128 : (n + 1) * 128, :].astype(f32)
        if i != j:
            n_ref[j * 128 : (j + 1) * 128, i * 128 : (i + 1) * 128] = block.T
        elif i == 3:
            corner = block[127:128, :]
            got = corner[:, 0:1] + corner[:, 1:2] + corner[:, 2:3]
            block = jnp.where((row == 127) & (col < 3), block.T, block)
        n_ref[i * 128 : (i + 1) * 128, j * 128 : (j + 1) * 128] = block
    chain(n_ref, dev, w_ref, v_ref, m_ref, r_ref, lambda v: v.astype(bf16), dot1)
    eye = lax.broadcasted_iota(jnp.int32, (B, B), 0) == lax.broadcasted_iota(jnp.int32, (B, B), 1)
    root[...] = got * (jnp.where(eye, 1.0, 0.0) - dev[...])
    total = exchanged(*e3)
    graft[...] = jnp.broadcast_to(jnp.sqrt(total[1:2, :] / jnp.maximum(total[0:1, :], 1.0)), graft.shape)

    for s in range(2):
        @pl.when(2 * c + s != x)
        def _():
            ref = pbox.at[:, s * B : (s + 1) * B]
            remote(ref, ref, o_s.at[0], o_r.at[s], other).wait_recv()

    @pl.when(c == 0)
    def _():
        for t in cross(half):
            t.wait_send()

    @pl.when(c == 1)
    def _():
        for t in cross(0):
            t.wait_send()

    for there in range(2):
        @pl.when((forwards & (kappa == c)) == bool(there))
        def _():
            ref = pack.at[0 : (MID - there) * PIECE]
            remote(ref, ref, a_s, a_r, other).wait_send()

    for r in range(2):
        @pl.when(2 * c + r != x)
        def _():
            rows_to(r).wait_send()

    @pl.when(forwards)
    def _():
        ref = stage.at[1 : NZ * NX]
        remote(ref, ref, b_s, b_r, other).wait_send()

    for e in (e1, e2, e3):
        sent(*e)


N_GRAD = 6 + 15
N_ROOT = 5


def step_kernel(owners, act, cot, pbox, root, graft, g, dev, scale, own, src, own_sem, *refs):
    grad, spare, rest = refs[:N_GRAD], refs[N_GRAD : N_GRAD + N_ROOT], refs[N_GRAD + N_ROOT :]
    load = pltpu.make_async_copy(owners, own, own_sem)
    load.start()

    def table():
        load.wait()

        def entry(d, carry):
            place = jnp.int32(0)
            for b in range(NB):
                at = (b // 2) * 4 + b % 2
                o = own[b]
                place = jnp.where(o == d, at, place)
                place = jnp.where(o + 1 - 2 * (o % 2) == d, at + 2, place)
            src[d] = place
            return carry

        lax.fori_loop(0, NZ * NX, entry, 0)

    gradient_stage(act, cot, g, table, *grad)
    statistic_stage(g, scale, spare[0], spare[1])
    finish_stage(src, g, dev, scale, spare, pbox, root, graft, *rest)


def step(owners, act, cot):
    dma = pltpu.SemaphoreType.DMA
    vmem = pltpu.VMEM
    in_vmem = pl.BlockSpec(memory_space=pltpu.VMEM)
    return pl.pallas_call(
        step_kernel,
        out_shape=(
            jax.ShapeDtypeStruct((B // NX, CB * B), f32),
            jax.ShapeDtypeStruct((B, B), f32),
            jax.ShapeDtypeStruct((8, 128), f32),
        ),
        in_specs=[pl.BlockSpec(memory_space=pltpu.HBM)] * 3,
        out_specs=(in_vmem,) * 3,
        scratch_shapes=[
            vmem((B, B), f32), vmem((B, B), f32), vmem((8, 128), f32),
            pltpu.SMEM((NB,), jnp.int32), pltpu.SMEM((NZ * NX,), jnp.int32), pltpu.SemaphoreType.DMA,
            vmem((NZ, 2, NY, TY, B), bf16),
            vmem((NZ, 2, T, B), bf16),
            vmem((TY, NZ * B), bf16),
            vmem((T, CB * B), bf16),
            vmem((4, B // 4, B), f32),
            vmem((4, B // 4, B), f32),
            dma((2,)),
            dma((2,)), dma((2,)),
            dma, dma((NZ,)),
            dma, dma((NY * 4,)),
            dma, dma((16,)),
            dma, dma((8,)),
            dma((2,)), dma((NY * 4,)),
            dma((4,)), dma((4,)),
            *[vmem((B, B), f32)] * N_ROOT,
            vmem((MID, PIECE, 128), bf16),
            vmem((B, B), bf16), vmem((B, B), bf16), vmem((B, B), bf16), vmem((B, B), bf16),
            vmem((8, 128), f32),
            vmem((MID * PIECE, 128), bf16),
            vmem((NZ * NX, PIECE, 128), bf16),
            vmem((NZ * NX, PIECE, 128), bf16),
            vmem((B, B), f32),
            vmem((2, 128, B), f32),
            vmem((8, 8, 128), f32), vmem((8, 8, 128), f32), vmem((8, 8, 128), f32),
            dma((3,)), dma((3,)),
            dma, dma, dma, dma,
            dma((2,)), dma((2,)),
            dma, dma, dma, dma, dma, dma,
        ],
        compiler_params=pltpu.CompilerParams(
            collective_id=0, has_side_effects=True, vmem_limit_bytes=52 * 2**20
        ),
        name="step",
    )(owners, act, cot)


def output_kernel(pbox, root_in, graft, update, root, factor, sem):
    copy = pltpu.make_async_copy(root_in, root, sem)
    copy.start()
    update[...] = (graft[0:1, 0:1] * pbox[...]).astype(bf16)
    factor[...] = graft[0:1, 0:1]
    copy.wait()


def outputs(pbox, root, graft):
    vmem = pl.BlockSpec(memory_space=pltpu.VMEM)
    anyw = pl.BlockSpec(memory_space=pl.ANY)
    return pl.pallas_call(
        output_kernel,
        out_shape=(
            jax.ShapeDtypeStruct((B // NX, CB * B), bf16),
            jax.ShapeDtypeStruct((B, B), f32),
            jax.ShapeDtypeStruct((1, 1), f32),
        ),
        in_specs=[vmem, anyw, vmem],
        out_specs=(vmem, anyw, vmem),
        scratch_shapes=[pltpu.SemaphoreType.DMA],
        compiler_params=pltpu.CompilerParams(vmem_limit_bytes=8 * 2**20),
        name="outputs",
    )(pbox, root, graft)


def on_device(act, cot, owners):
    update, root, graft = outputs(*step(owners, act, cot))
    return update, root, graft.reshape(())


def solution(mesh):
    finer = Mesh(mesh.devices.reshape(NZ, NX, NY, 2), ("z", "x", "y", "c"))
    dp, mp = ("z", "x"), ("y", "c")
    return jax.shard_map(
        on_device,
        mesh=finer,
        in_specs=(P(dp, None), P(dp, mp), P()),
        out_specs=(P(dp, mp), P(dp, mp), P()),
        check_vma=False,
    )
```

time: 95.4 us -> 83.4 us (0.87); the launches traced: 93.7 us -> 83.2 us
  Pallas kernels: 89.9 us -> 80.8 us
  other arithmetic: 1.28 us -> 0 us
    pallas_call x1, Pallas kernels: 87.5 us -> 79.1 us  [step(): pl.pallas_call(step_kernel, out_shape=(jax.ShapeDtypeStruct((B // NX, CB...]
    slice x1 -> x0, local copies, waits for them, and re-layouts: 1.19 us -> none  [on_device(): return (update, root, graft[0, 0])]
    unnamed x2 -> x4, local copies, waits for them, and re-layouts: 0.64 us -> 1.6 us
where the time goes in v3:
time: 83.4 us; the launch traced here: 83.2 us
  Pallas kernels  80.8 us (97%)
  local copies, waits for them, and re-layouts  1.6 us (2%)
    pallas_call x1, Pallas kernels, step(): pl.pallas_call(step_kernel, out_shape=(jax.ShapeDtypeStruct((B // NX, CB...  79.1 us
    pallas_call x1, Pallas kernels, outputs(): pl.pallas_call(output_kernel, out_shape=(jax.ShapeDtypeStruct((B // NX, C...  1.68 us

profile of v3, /device:TPU:1, one launch (start us, length us, event | category | flops | bytes accessed | tf_op | source)
XLA Modules:
  0.0 83.2 jit_solution(9059545985466163278)
XLA Ops:
  0.6 0.0 copy-start
  0.6 0.9 %copy-done = bf16[128,1024]{1,0:T(8,128)(2,1)S(1)} copy-done((bf16[128,1024]{1,0:T(8,128)(2,1)S(1)}, bf16[128,1024]{1,0:T(8,128)(2,1)}, u32[]{:S(2)}) %copy-start) | copy-done | bytes 262168
  1.6 0.0 copy-start.1
  1.6 0.7 copy-done.1
  2.2 79.1 %step.1 = (f32[128,1024]{1,0:T(8,128)S(1)}, f32[512,512]{1,0:T(8,128)S(1)}, f32[8,128]{1,0:T(8,128)S(1)}) custom-call(s32[16]{0:T(128)S(1)} %copy-done.1, bf16[128,4096]{1,0:T(8,128)(2,1)} %act.1, bf16[128,1024]{1,0:T(8,128)(2,1)S(1)} %copy-done), custom_call_target="tpu_custom_call" | custom-call | tf_op jit(solution)/shard_map/step/pallas_call | solution.py:564
  81.4 1.7 %outputs.1 = (bf16[128,1024]{1,0:T(8,128)(2,1)}, f32[512,512]{1,0:T(8,128)}, f32[1,1]{1,0:T(1,128)}) custom-call(f32[128,1024]{1,0:T(8,128)S(1)} %get-tuple-element.9.pbox, f32[512,512]{1,0:T(8,128)S(1)} %get-tuple-element.10.root_in, f32[8,128]{1,0:T(8,128)S(1)} %get-tuple-element.11.graft), custom_call_target="tpu_custom_call" | custom-call | tf_op jit(solution)/shard_map/outputs/pallas_call | solution.py:623
Async XLA Ops:
  0.6 1.0 %copy-start = (bf16[128,1024]{1,0:T(8,128)(2,1)S(1)}, bf16[128,1024]{1,0:T(8,128)(2,1)}, u32[]{:S(2)}) copy-start(bf16[128,1024]{1,0:T(8,128)(2,1)} %cot.1) | copy-start | bytes 786436
  1.6 0.7 copy-start.1

commit v4 on v3

--- a/solution.py
+++ b/solution.py
@@ -116,12 +116,14 @@
     def at_y(q):
         return (y + NY + offsets[q]) % NY
 
-    def y_move(step, direction, back):
+    def y_move(step, direction, back, part):
         k = (y + NY - direction * (step - 1 + back)) % NY
-        part = slice(0, NZ) if step < NY // 2 else halves[direction < 0]
-        ref = abuf.at[part, xs, k]
-        i = (step - 1) * 2 + (direction > 0)
+        ref = abuf.at[halves[part], xs, k]
+        i = (step - 1) * 4 + part * 2 + (direction > 0)
         return remote(ref, ref, ar_s, ar_r.at[i], (z, x, (y + NY + direction) % NY, c))
+
+    def y_parts(step, direction):
+        return (0, 1) if step < NY // 2 else (int(direction < 0),)
 
     def x_move(q, s, direction):
         ref = abuf.at[:, s, at_y(q)]
@@ -148,13 +150,16 @@
     def y_step(step):
         @pl.when(active)
         def _():
-            for d in (1, -1):
-                y_move(step, d, 1).wait_recv()
-                if step + 1 <= NY // 2:
-                    y_move(step + 1, d, 0).start()
-                if step < NY // 2:
-                    x_start(2 * step - (d > 0))
-            if step == NY // 2:
+            for part in range(2):
+                for d in (1, -1):
+                    if part in y_parts(step, d):
+                        y_move(step, d, 1, part).wait_recv()
+                    if step < NY // 2 and part in y_parts(step + 1, d):
+                        y_move(step + 1, d, 0, part).start()
+            if step < NY // 2:
+                x_start(2 * step - 1)
+                x_start(2 * step)
+            else:
                 x_start(NY - 1)
 
     for o in range(2):
@@ -168,8 +173,9 @@
         for d in range(NZ):
             ref = abuf.at[(z + NZ - d) % NZ, xs, y]
             remote(ref, ref, a1_s, a1_r.at[d], (z, x, y, c)).wait_recv()
-        for d in (1, -1):
-            y_move(1, d, 0).start()
+        for part in range(2):
+            for d in (1, -1):
+                y_move(1, d, 0, part).start()
         x_start(0)
 
     y_step(1)
@@ -177,15 +183,15 @@
     c_step(1)
     y_step(2)
     x_relay(1)
+    c_step(2)
     x_relay(2)
     y_step(3)
-    c_step(2)
     x_relay(3)
     x_relay(4)
     y_step(4)
+    c_step(3)
     x_relay(5)
     x_relay(6)
-    c_step(3)
     x_relay(7)
     c_step(4)
     for s in range(2):
@@ -204,9 +210,7 @@
         lhs = abuf[:, :, :, :, r * rows : (r + 1) * rows].reshape(NZ * 2 * T, rows)
         part = lax.dot_general(lhs, cot_all, (((0,), (0,)), ((), ())), preferred_element_type=f32)
         psend[r] = part * (1.0 / 64.0)
-        if r:
-            pcopy(r - 1).start()
-    pcopy(3).start()
+        pcopy(r).start()
 
     for h in range(2):
         @pl.when(2 * c + h != x)
@@ -249,7 +253,20 @@
 
 
 def dot1(a, b):
-    return jnp.dot(a, b, preferred_element_type=f32)
+    return jnp.dot(a[0], b[0], preferred_element_type=f32)
+
+
+def symmetric(ref, top, low):
+    half = B // 2
+    ref[:half, :] = top
+    ref[half:, :half] = top[:, half:].T
+    ref[half:, half:] = low
+
+
+def product_into(ref, a, b, dot):
+    half = B // 2
+    top = dot([v[:half, :] for v in a], b)
+    symmetric(ref, top, dot([v[half:, :] for v in a], [v[:, half:] for v in b]))
 
 
 SCALE0 = 1.25**3
@@ -261,15 +278,21 @@
     ridge = 0.1 * (jnp.sum(g * g, keepdims=True) / B + 1.0)
     eye = lax.broadcasted_iota(jnp.int32, (B, B), 0) == lax.broadcasted_iota(jnp.int32, (B, B), 1)
 
+    half = B // 2
+
     @pl.when(c == 0)
     def _():
+        dims = (((1,), (1,)), ((), ()))
         gg = split(g_ref[...])
-        w_ref[...] = dot3(gg, gg, (((1,), (1,)), ((), ())))
+        low = [v[half:, :] for v in gg]
+        symmetric(w_ref, dot3([v[:half, :] for v in gg], gg, dims), dot3(low, low, dims))
 
     @pl.when(c == 1)
     def _():
+        dims = (((0,), (0,)), ((), ()))
         gg = split(g_ref[...])
-        w_ref[...] = dot3(gg, gg, (((0,), (0,)), ((), ())))
+        low = [v[:, half:] for v in gg]
+        symmetric(w_ref, dot3([v[:, :half] for v in gg], gg, dims), dot3(low, low, dims))
 
     stat = w_ref[...] + jnp.where(eye, ridge, 0.0)
     w_ref[...] = stat
@@ -281,17 +304,18 @@
 def chain(n_ref, d_ref, w_ref, v_ref, m_ref, r_ref, parts, dot):
     def advance(src, dst):
         n = parts(src[...])
-        w_ref[...] = dot(n, n)
-        v_ref[...] = dot(n, parts(w_ref[...]))
-        u = src[...] - 2.0 * w_ref[...] + v_ref[...]
-        v_ref[...] = u
-        left = parts(w_ref[...] - 2.0 * src[...])
-        dst[...] = (1.25**4) * (v_ref[...] + dot(left, parts(v_ref[...])))
+        product_into(w_ref, n, n, dot)
+        product_into(v_ref, n, parts(w_ref[...]), dot)
+        v_ref[...] = src[...] - 2.0 * w_ref[...] + v_ref[...]
+        product_into(dst, parts(w_ref[...] - 2.0 * src[...]), parts(v_ref[...]), dot)
+        dst[...] = (1.25**4) * (v_ref[...] + dst[...])
 
     advance(n_ref, m_ref)
-    r_ref[...] = n_ref[...] + m_ref[...] - dot(parts(n_ref[...]), parts(m_ref[...]))
+    product_into(r_ref, parts(n_ref[...]), parts(m_ref[...]), dot)
+    r_ref[...] = n_ref[...] + m_ref[...] - r_ref[...]
     advance(m_ref, n_ref)
-    d_ref[...] = r_ref[...] + n_ref[...] - dot(parts(r_ref[...]), parts(n_ref[...]))
+    product_into(d_ref, parts(r_ref[...]), parts(n_ref[...]), dot)
+    d_ref[...] = r_ref[...] + n_ref[...] - d_ref[...]
 
 
 PAIRS = [(i, j) for i in range(4) for j in range(i, 4)]
@@ -357,8 +381,9 @@
     def is_me(k):
         return (k == k_me) & forwards & (kappa == c)
 
+    far_first = (4, 3, 5, 2, 6, 1, 7, 0)
     for t in range(MID):
-        k = (t + 2 * z) % MID
+        k = (2 * (z + far_first[t // 2]) + t % 2) % MID
 
         @pl.when(jnp.logical_not(is_me(k)))
         def _():
@@ -398,31 +423,19 @@
     def _():
         t_ref[...] = g[...] - dot3(split(g[...]), (dhi[...], dlo[...]))
 
-    def leg_b(t):
-        d = (z * NX + x + t) % (NZ * NX)
-        return remote(stage.at[t], bbox.at[k_me], b_s, b_r, (d // NX, d % NX, y, c))
-
-    @pl.when(forwards)
-    def _():
-        for there in range(2):
-            @pl.when((kappa == c) == bool(there))
-            def _():
-                ref = abox.at[0 : NZ * NX - there]
-                remote(ref, ref, a_s, a_r, other).wait_recv()
-        for t in range(NZ * NX):
-            piece = abox[src[(z * NX + x + t) % (NZ * NX)]]
-            if t:
-                stage[t] = piece
-            else:
-                bbox[k_me] = piece
     @pl.when(c == 0)
     def _():
-        for t in cross(0):
-            t.wait_recv()
+        high, low, scales = cross(0)
+        u = t_ref[:half, :]
+        uh, ul = split(u)
+        high.wait_recv()
+        first = jnp.dot(uh, phi[...], preferred_element_type=f32) + jnp.dot(ul, phi[...], preferred_element_type=f32)
+        low.wait_recv()
+        scales.wait_recv()
         factor = scale[0:1, 0:1] * pscale[0:1, 0:1]
-        for r in range(2):
-            u = t_ref[r * 128 : (r + 1) * 128, :]
-            pout[r] = factor * (u - dot3(split(u), (phi[...], plo[...])))
+        p = factor * (u - (first + jnp.dot(uh, plo[...], preferred_element_type=f32)))
+        pout[0] = p[:128, :]
+        pout[1] = p[128:, :]
 
     @pl.when(c == 1)
     def _():
@@ -445,17 +458,35 @@
     e3 = (box3, z, NZ, lambda i: (i, x, y, c), e3_s, e3_r)
     exchange(e1[0], value, *e1[1:])
 
-    @pl.when(forwards)
-    def _():
-        for t in range(1, NZ * NX):
-            leg_b(t).start()
-
 
     def rows_to(r):
         return remote(
             pout.at[r], pbox.at[:, pl.ds(pl.multiple_of(xs * B, B), B)], o_s.at[r], o_r.at[xs], (z, 2 * c + r, y, kappa)
         )
 
+    def place_b(t):
+        return (z + far_first[t // NX]) % NZ, (x + NX - 1 - t % NX) % NX
+
+    def leg_b(t):
+        zd, xd = place_b(t)
+        return remote(stage.at[t], bbox.at[k_me], b_s, b_r, (zd, xd, y, c))
+
+    @pl.when(forwards)
+    def _():
+        for there in range(2):
+            @pl.when((kappa == c) == bool(there))
+            def _():
+                ref = abox.at[0 : NZ * NX - there]
+                remote(ref, ref, a_s, a_r, other).wait_recv()
+        for t in range(NZ * NX):
+            zd, xd = place_b(t)
+            piece = abox[src[zd * NX + xd]]
+            if t < NZ * NX - 1:
+                stage[t] = piece
+            else:
+                bbox[k_me] = piece
+        for t in range(NZ * NX - 1):
+            leg_b(t).start()
     for r in range(2):
         @pl.when(2 * c + r != x)
         def _():
@@ -486,7 +517,7 @@
             got = corner[:, 0:1] + corner[:, 1:2] + corner[:, 2:3]
             block = jnp.where((row == 127) & (col < 3), block.T, block)
         n_ref[i * 128 : (i + 1) * 128, j * 128 : (j + 1) * 128] = block
-    chain(n_ref, dev, w_ref, v_ref, m_ref, r_ref, lambda v: v.astype(bf16), dot1)
+    chain(n_ref, dev, w_ref, v_ref, m_ref, r_ref, lambda v: (v.astype(bf16),), dot1)
     eye = lax.broadcasted_iota(jnp.int32, (B, B), 0) == lax.broadcasted_iota(jnp.int32, (B, B), 1)
     root[...] = got * (jnp.where(eye, 1.0, 0.0) - dev[...])
     total = exchanged(*e3)
@@ -521,7 +552,7 @@
 
     @pl.when(forwards)
     def _():
-        ref = stage.at[1 : NZ * NX]
+        ref = stage.at[0 : NZ * NX - 1]
         remote(ref, ref, b_s, b_r, other).wait_send()
 
     for e in (e1, e2, e3):
@@ -584,7 +615,7 @@
             dma, dma((NZ,)),
             dma, dma((NY * 4,)),
             dma, dma((16,)),
-            dma, dma((8,)),
+            dma, dma((16,)),
             dma((2,)), dma((NY * 4,)),
             dma((4,)), dma((4,)),
             *[vmem((B, B), f32)] * N_ROOT,

time: 83.4 us -> 82.8 us (level)
  Pallas kernels: 80.8 us -> 79.6 us
    pallas_call x1, Pallas kernels: 79.1 us -> 77.9 us  [step(): pl.pallas_call(step_kernel, out_shape=(jax.ShapeDtypeStruct((B // NX, CB...]
where the time goes in v4:
time: 82.8 us; the launch traced here: 82 us
  Pallas kernels  79.6 us (96%)
  local copies, waits for them, and re-layouts  1.6 us (2%)
    pallas_call x1, Pallas kernels, step(): pl.pallas_call(step_kernel, out_shape=(jax.ShapeDtypeStruct((B // NX, CB...  77.9 us
    pallas_call x1, Pallas kernels, outputs(): pl.pallas_call(output_kernel, out_shape=(jax.ShapeDtypeStruct((B // NX, C...  1.68 us

profile of v4, /device:TPU:1, one launch (start us, length us, event | category | flops | bytes accessed | tf_op | source)
XLA Modules:
  0.0 82.0 jit_solution(17454800413867875488)
XLA Ops:
  0.6 0.0 copy-start
  0.6 0.9 %copy-done = bf16[128,1024]{1,0:T(8,128)(2,1)S(1)} copy-done((bf16[128,1024]{1,0:T(8,128)(2,1)S(1)}, bf16[128,1024]{1,0:T(8,128)(2,1)}, u32[]{:S(2)}) %copy-start) | copy-done | bytes 262168
  1.6 0.0 copy-start.1
  1.6 0.7 copy-done.1
  2.2 77.9 %step.1 = (f32[128,1024]{1,0:T(8,128)S(1)}, f32[512,512]{1,0:T(8,128)S(1)}, f32[8,128]{1,0:T(8,128)S(1)}) custom-call(s32[16]{0:T(128)S(1)} %copy-done.1, bf16[128,4096]{1,0:T(8,128)(2,1)} %act.1, bf16[128,1024]{1,0:T(8,128)(2,1)S(1)} %copy-done), custom_call_target="tpu_custom_call" | custom-call | tf_op jit(solution)/shard_map/step/pallas_call | solution.py:595
  80.1 1.7 %outputs.1 = (bf16[128,1024]{1,0:T(8,128)(2,1)}, f32[512,512]{1,0:T(8,128)}, f32[1,1]{1,0:T(1,128)}) custom-call(f32[128,1024]{1,0:T(8,128)S(1)} %get-tuple-element.9.pbox, f32[512,512]{1,0:T(8,128)S(1)} %get-tuple-element.10.root_in, f32[8,128]{1,0:T(8,128)S(1)} %get-tuple-element.11.graft), custom_call_target="tpu_custom_call" | custom-call | tf_op jit(solution)/shard_map/outputs/pallas_call | solution.py:654
Async XLA Ops:
  0.6 1.0 %copy-start = (bf16[128,1024]{1,0:T(8,128)(2,1)S(1)}, bf16[128,1024]{1,0:T(8,128)(2,1)}, u32[]{:S(2)}) copy-start(bf16[128,1024]{1,0:T(8,128)(2,1)} %cot.1) | copy-start | bytes 786436
  1.6 0.7 copy-start.1

commit v5 on v4

--- a/solution.py
+++ b/solution.py
@@ -183,12 +183,12 @@
     c_step(1)
     y_step(2)
     x_relay(1)
+    y_step(3)
     c_step(2)
     x_relay(2)
-    y_step(3)
+    y_step(4)
     x_relay(3)
     x_relay(4)
-    y_step(4)
     c_step(3)
     x_relay(5)
     x_relay(6)

time: 82.8 us -> 81.8 us (0.988)
  Pallas kernels: 79.6 us -> 78.5 us
    pallas_call x1, Pallas kernels: 77.9 us -> 76.8 us  [step(): pl.pallas_call(step_kernel, out_shape=(jax.ShapeDtypeStruct((B // NX, CB...]
where the time goes in v5:
time: 81.8 us; the launch traced here: 80.9 us
  Pallas kernels  78.5 us (96%)
  local copies, waits for them, and re-layouts  1.6 us (2%)
    pallas_call x1, Pallas kernels, step(): pl.pallas_call(step_kernel, out_shape=(jax.ShapeDtypeStruct((B // NX, CB...  76.8 us
    pallas_call x1, Pallas kernels, outputs(): pl.pallas_call(output_kernel, out_shape=(jax.ShapeDtypeStruct((B // NX, C...  1.68 us

profile of v5, /device:TPU:1, one launch (start us, length us, event | category | flops | bytes accessed | tf_op | source)
XLA Modules:
  0.0 80.9 jit_solution(2178542500287736041)
XLA Ops:
  0.6 0.0 copy-start
  0.6 0.9 %copy-done = bf16[128,1024]{1,0:T(8,128)(2,1)S(1)} copy-done((bf16[128,1024]{1,0:T(8,128)(2,1)S(1)}, bf16[128,1024]{1,0:T(8,128)(2,1)}, u32[]{:S(2)}) %copy-start) | copy-done | bytes 262168
  1.6 0.0 copy-start.1
  1.6 0.7 copy-done.1
  2.2 76.8 %step.1 = (f32[128,1024]{1,0:T(8,128)S(1)}, f32[512,512]{1,0:T(8,128)S(1)}, f32[8,128]{1,0:T(8,128)S(1)}) custom-call(s32[16]{0:T(128)S(1)} %copy-done.1, bf16[128,4096]{1,0:T(8,128)(2,1)} %act.1, bf16[128,1024]{1,0:T(8,128)(2,1)S(1)} %copy-done), custom_call_target="tpu_custom_call" | custom-call | tf_op jit(solution)/shard_map/step/pallas_call | solution.py:595
  79.1 1.7 %outputs.1 = (bf16[128,1024]{1,0:T(8,128)(2,1)}, f32[512,512]{1,0:T(8,128)}, f32[1,1]{1,0:T(1,128)}) custom-call(f32[128,1024]{1,0:T(8,128)S(1)} %get-tuple-element.9.pbox, f32[512,512]{1,0:T(8,128)S(1)} %get-tuple-element.10.root_in, f32[8,128]{1,0:T(8,128)S(1)} %get-tuple-element.11.graft), custom_call_target="tpu_custom_call" | custom-call | tf_op jit(solution)/shard_map/outputs/pallas_call | solution.py:654
Async XLA Ops:
  0.6 1.0 %copy-start = (bf16[128,1024]{1,0:T(8,128)(2,1)S(1)}, bf16[128,1024]{1,0:T(8,128)(2,1)}, u32[]{:S(2)}) copy-start(bf16[128,1024]{1,0:T(8,128)(2,1)} %cot.1) | copy-start | bytes 786436
  1.6 0.7 copy-start.1

commit v6 on v5

--- a/solution.py
+++ b/solution.py
@@ -185,8 +185,8 @@
     x_relay(1)
     y_step(3)
     c_step(2)
+    y_step(4)
     x_relay(2)
-    y_step(4)
     x_relay(3)
     x_relay(4)
     c_step(3)
@@ -423,6 +423,7 @@
     def _():
         t_ref[...] = g[...] - dot3(split(g[...]), (dhi[...], dlo[...]))
 
+    sum_g = 0.5 * jnp.sum(g[...] * g[...], keepdims=True)
     @pl.when(c == 0)
     def _():
         high, low, scales = cross(0)
@@ -449,7 +450,6 @@
 
     sum_p = jnp.sum(pout[...] * pout[...], axis=0)
     sum_p = jnp.sum(sum_p, keepdims=True)
-    sum_g = 0.5 * jnp.sum(g[...] * g[...], keepdims=True)
     row8 = lax.broadcasted_iota(jnp.int32, (8, 128), 0)
     value = jnp.where(row8 == 0, sum_p, jnp.where(row8 == 1, sum_g, 0.0))
 

time: 81.8 us -> 81 us (level)
  no operation moved by 1% of the time
where the time goes in v6:
time: 81 us; the launch traced here: 80.6 us
  Pallas kernels  78.2 us (97%)
  local copies, waits for them, and re-layouts  1.6 us (2%)
  between operations  0.81 us (1%)
    pallas_call x1, Pallas kernels, step(): pl.pallas_call(step_kernel, out_shape=(jax.ShapeDtypeStruct((B // NX, CB...  76.6 us
    pallas_call x1, Pallas kernels, outputs(): pl.pallas_call(output_kernel, out_shape=(jax.ShapeDtypeStruct((B // NX, C...  1.68 us

profile of v6, /device:TPU:1, one launch (start us, length us, event | category | flops | bytes accessed | tf_op | source)
XLA Modules:
  0.0 80.6 jit_solution(15791323462132085276)
XLA Ops:
  0.6 0.0 copy-start
  0.6 0.9 %copy-done = bf16[128,1024]{1,0:T(8,128)(2,1)S(1)} copy-done((bf16[128,1024]{1,0:T(8,128)(2,1)S(1)}, bf16[128,1024]{1,0:T(8,128)(2,1)}, u32[]{:S(2)}) %copy-start) | copy-done | bytes 262168
  1.6 0.0 copy-start.1
  1.6 0.7 copy-done.1
  2.2 76.6 %step.1 = (f32[128,1024]{1,0:T(8,128)S(1)}, f32[512,512]{1,0:T(8,128)S(1)}, f32[8,128]{1,0:T(8,128)S(1)}) custom-call(s32[16]{0:T(128)S(1)} %copy-done.1, bf16[128,4096]{1,0:T(8,128)(2,1)} %act.1, bf16[128,1024]{1,0:T(8,128)(2,1)S(1)} %copy-done), custom_call_target="tpu_custom_call" | custom-call | tf_op jit(solution)/shard_map/step/pallas_call | solution.py:595
  78.8 1.7 %outputs.1 = (bf16[128,1024]{1,0:T(8,128)(2,1)}, f32[512,512]{1,0:T(8,128)}, f32[1,1]{1,0:T(1,128)}) custom-call(f32[128,1024]{1,0:T(8,128)S(1)} %get-tuple-element.9.pbox, f32[512,512]{1,0:T(8,128)S(1)} %get-tuple-element.10.root_in, f32[8,128]{1,0:T(8,128)S(1)} %get-tuple-element.11.graft), custom_call_target="tpu_custom_call" | custom-call | tf_op jit(solution)/shard_map/outputs/pallas_call | solution.py:654
Async XLA Ops:
  0.6 1.0 %copy-start = (bf16[128,1024]{1,0:T(8,128)(2,1)S(1)}, bf16[128,1024]{1,0:T(8,128)(2,1)}, u32[]{:S(2)}) copy-start(bf16[128,1024]{1,0:T(8,128)(2,1)} %cot.1) | copy-start | bytes 786436
  1.6 0.7 copy-start.1
